TPU v7x, 1024 devices: a whole 8x8x8 slice. The times are simulated.
1024 devices in a mesh: grp: 64 (over y_lo, z, core), sp: 16 (over x, y_hi).
Axes of the slice: x: 8, y: 8 (y_hi: 2, y_lo: 4; y = y_hi * 4 + y_lo), z: 8, core: 2. Of those that a mesh axis runs over, the one named last changes fastest.
Arguments:
- acts: bfloat16 [1024, 16, 16, 728], P('grp', 'sp'), may hold values from -6 to 6
- cotangent: bfloat16 [1024, 16, 16, 728], P(('grp', 'sp')), may hold values from -6 to 6
- depth_kernel: float32 [3, 3, 728], replicated, may hold values from -2 to 2
- point_weight: bfloat16 [728, 728], replicated, may hold values from -0.21875 to 0.21875
- batch_norm_gain: float32 [728], replicated, may hold values from 0.5 to 2
- norm_shift_bias: float32 [728], replicated, may hold values from -1 to 1
Outputs:
- block_out: bfloat16 [1024, 16, 16, 728], P(('grp', 'sp'))
- input_grad: bfloat16 [1024, 16, 16, 728], P('grp', 'sp')
- weight_grad: float32 [529984], P('sp')
All inputs are finite; a program needn't handle non-finite values.
Results may differ from a plain program's by a relative error of at most 0.018.
Values may be sent and summed in bfloat16 or wider, within the bound.
No kernel may reach another device: no remote copies, remote signals or barrier semaphores. Data moves between devices by JAX's collectives and lax.ppermute only.
A program may use at most 32 MiB of HBM per device.

v0:
```python
import jax
import jax.numpy as jnp
from jax import lax
from jax.sharding import PartitionSpec as P


def sent_to_all(shard, axis):
    copies = jnp.broadcast_to(shard, (lax.axis_size(axis), *shard.shape))
    return lax.all_to_all(copies, axis, split_axis=0, concat_axis=0, tiled=True)


def over_copies(shard, axis):
    return sent_to_all(shard, axis).sum(axis=0)


def together(arrays, axis):
    ends = [0]
    for a in arrays:
        ends.append(ends[-1] + a.size)
    total = over_copies(jnp.concatenate([a.ravel() for a in arrays]), axis)
    return tuple((total[b:e].reshape(a.shape) for a, b, e in zip(arrays, ends, ends[1:])))


def in_blocks(shard, dim, devices):
    shape = shard.shape
    parts = shard.reshape(*shape[:dim], devices, shape[dim] // devices, *shape[dim + 1 :])
    return jnp.moveaxis(parts, dim, 0)


def summed_on_arrival(shard, axis, dim):
    parts = in_blocks(shard, dim, lax.axis_size(axis))
    arrived = lax.all_to_all(parts, axis, split_axis=0, concat_axis=0, tiled=True)
    return arrived.astype(jnp.float32).sum(axis=0)


def sum_at_owner(shard, axis, dim):
    devices = lax.axis_size(axis)
    parts = lax.all_to_all(in_blocks(shard, dim, devices), axis, 0, 0, tiled=True)
    return jnp.sum(parts, axis=0)


def in_order(parts, dim):
    shape = list(parts.shape[1:])
    shape[dim] *= parts.shape[0]
    return jnp.moveaxis(parts, 0, dim).reshape(shape)


def gather_directly(shard, axis, dim):
    parts = sent_to_all(shard, axis)
    return in_order(parts, dim)


def depth_forward(field, filter_weight):
    rows = field.shape[1]
    cols = field.shape[2]
    padded = jnp.pad(field, ((0, 0), (1, 1), (1, 1), (0, 0)))
    total = jnp.zeros(field.shape, jnp.float32)
    for i in range(3):
        for j in range(3):
            total = total + padded[:, i : i + rows, j : j + cols, :] * filter_weight[i, j]
    return total


def depth_backward(field, filter_weight):
    rows = field.shape[1]
    cols = field.shape[2]
    padded = jnp.pad(field, ((0, 0), (1, 1), (1, 1), (0, 0)))
    total = jnp.zeros(field.shape, jnp.float32)
    for i in range(3):
        for j in range(3):
            total = (
                total
                + padded[:, 2 - i : 2 - i + rows, 2 - j : 2 - j + cols, :] * filter_weight[i, j]
            )
    return total


def body(acts, cotangent, depth_kernel, point_weight, batch_norm_gain, norm_shift_bias):
    channel_count = acts.shape[-1]
    sample_image = lax.all_to_all(acts, "sp", split_axis=0, concat_axis=1, tiled=True)
    input_single_precision = sample_image.astype(jnp.float32)
    hidden = jnp.maximum(input_single_precision, 0.0)
    depthed = depth_forward(hidden, depth_kernel).astype(jnp.bfloat16)
    flat_d = depthed.reshape(-1, channel_count)
    element_count = flat_d.shape[0] * lax.axis_size("sp")
    projected_output = jnp.dot(flat_d, point_weight, preferred_element_type=jnp.float32)
    total, squares = together(
        (jnp.sum(projected_output, axis=0), jnp.sum(projected_output * projected_output, axis=0)),
        "sp",
    )
    batch_mean = total / element_count
    var = squares / element_count - batch_mean * batch_mean
    inverse_deviation = lax.rsqrt(var + 1e-05)
    normalized_input = (projected_output - batch_mean) * inverse_deviation
    block_out = (
        (
            input_single_precision.reshape(-1, channel_count)
            + batch_norm_gain * normalized_input
            + norm_shift_bias
        )
        .astype(jnp.bfloat16)
        .reshape(sample_image.shape)
    )
    gfloat = cotangent.astype(jnp.float32).reshape(-1, channel_count)
    scaled_output = gfloat * batch_norm_gain
    leading_layer, second_layer = together(
        (jnp.sum(scaled_output, axis=0), jnp.sum(scaled_output * normalized_input, axis=0)), "sp"
    )
    projected_gradient = (
        inverse_deviation
        * (
            scaled_output
            - leading_layer / element_count
            - normalized_input * (second_layer / element_count)
        )
    ).astype(jnp.bfloat16)
    local_weight = jnp.dot(
        flat_d.T, projected_gradient, preferred_element_type=jnp.float32
    ).reshape(-1)
    ddepth = jnp.dot(
        projected_gradient, point_weight.T, preferred_element_type=jnp.float32
    ).reshape(sample_image.shape)
    dhidden = depth_backward(ddepth, depth_kernel)
    dinput = (
        gfloat.reshape(sample_image.shape) + jnp.where(sample_image > 0, dhidden, 0.0)
    ).astype(jnp.bfloat16)
    input_grad = lax.all_to_all(dinput, "sp", split_axis=1, concat_axis=0, tiled=True)
    slices = summed_on_arrival(local_weight.astype(jnp.bfloat16), "sp", 0)
    span = slices.shape[0]
    groups = lax.axis_size("grp")
    piece = (span + groups - 1) // groups
    padded = jnp.pad(slices, (0, piece * groups - span))
    summed = sum_at_owner(padded, "grp", 0)
    whole = gather_directly(summed, "grp", 0)
    weight_grad = whole[:span]
    return (block_out, input_grad, weight_grad)


def solution(mesh):
    in_specs = (P("grp", "sp", None, None), P(("grp", "sp"), None, None, None), P(), P(), P(), P())
    out_specs = (P(("grp", "sp"), None, None, None), P("grp", "sp", None, None), P("sp"))
    return jax.shard_map(body, mesh=mesh, in_specs=in_specs, out_specs=out_specs, check_vma=False)
```

profile of v0, /device:TPU:1, one launch (start us, length us, event | category | flops | bytes accessed | tf_op | source)
XLA Modules:
  0.0 213.4 jit_solution(9073928396136806409)
XLA Ops:
  0.6 13.3 %all-to-all-start = ((bf16[16,1,16,728]{3,2,1,0:T(8,128)(2,1)}), bf16[16,1,16,728]{3,2,1,0:T(8,128)(2,1)S(1)}, u32[]{:S(2)}, u32[]{:S(2)}) async-start(bf16[16,1,16,728]{3,2,1,0:T(8,128)(2,1)} %param.6), calls=%async_computation | async-start | bytes 786432 | tf_op jit(solution)/shard_map/all_to_all | solution.py:80
  13.9 0.9 slice_reduce_fusion.8
  14.9 14.2 %all-to-all-done = bf16[16,1,16,728]{3,2,1,0:T(8,128)(2,1)S(1)} async-done(((bf16[16,1,16,728]{3,2,1,0:T(8,128)(2,1)}), bf16[16,1,16,728]{3,2,1,0:T(8,128)(2,1)S(1)}, u32[]{:S(2)}, u32[]{:S(2)}) %all-to-all-start) | async-done | bytes 372768 | tf_op jit(solution)/shard_map/all_to_all | solution.py:80
  29.8 0.8 fusion.40
  31.4 3.5 %all-to-all-start.1 = ((f32[16,1,1456]{2,1,0:T(1,128)}), f32[16,1,1456]{2,1,0:T(1,128)S(1)}, u32[]{:S(2)}, u32[]{:S(2)}) async-start(f32[16,1,1456]{2,1,0:T(1,128)} %broadcast_in_dim.7), calls=%async_computation.1 | async-start | bytes 196608 | tf_op jit(solution)/shard_map/all_to_all | solution.py:9
  35.2 11.9 %all-to-all-done.1 = f32[16,1,1456]{2,1,0:T(1,128)S(1)} async-done(((f32[16,1,1456]{2,1,0:T(1,128)}), f32[16,1,1456]{2,1,0:T(1,128)S(1)}, u32[]{:S(2)}, u32[]{:S(2)}) %all-to-all-start.1) | async-done | bytes 93216 | tf_op jit(solution)/shard_map/all_to_all | solution.py:9
  48.5 3.7 %all-to-all-start.2 = ((f32[16,1,1456]{2,1,0:T(1,128)}), f32[16,1,1456]{2,1,0:T(1,128)S(1)}, u32[]{:S(2)}, u32[]{:S(2)}) async-start(f32[16,1,1456]{2,1,0:T(1,128)} %broadcast_in_dim.8), calls=%async_computation.2 | async-start | bytes 196608 | tf_op jit(solution)/shard_map/all_to_all | solution.py:9
  52.2 1.0 bitcast_convert_fusion
  53.2 2.3 %copy.41 = f32[256,728]{0,1:T(8,128)} copy(f32[256,728]{1,0:T(8,128)} %bitcast.37) | data formatting | bytes 1490944 | tf_op jit(solution)/shard_map/convert_element_type | solution.py:81
  55.5 8.7 %all-to-all-done.2 = f32[16,1,1456]{2,1,0:T(1,128)S(1)} async-done(((f32[16,1,1456]{2,1,0:T(1,128)}), f32[16,1,1456]{2,1,0:T(1,128)S(1)}, u32[]{:S(2)}, u32[]{:S(2)}) %all-to-all-start.2) | async-done | bytes 93216 | tf_op jit(solution)/shard_map/all_to_all | solution.py:9
  64.3 2.5 %multiply_convert_fusion = (bf16[256,728]{0,1:T(8,128)(2,1)S(1)}, bf16[256,728]{0,1:T(8,128)(2,1)}) fusion(f32[256,728]{0,1:T(8,128)S(1)} %copy.44, f32[256,728]{0,1:T(8,128)S(1)} %get-tuple-element.35, f32[728]{0:T(1024)S(1)} %get-tuple-element.32, f32[728]{0:T(1024)S(1)} %get-tuple-element.31, f32[728]{0:T(1024)S(1)} %get-tuple-element.34, ...), kind=kLoop, calls=%fused_computation.56 | loop fusion | flops 2236416 | bytes 2999360 | tf_op jit(solution)/shard_map/convert_element_type | solution.py:116
  66.9 0.7 copy-done.7
  68.1 3.4 %reshape.172 = bf16[529984]{0:T(1024)(128)(2,1)} reshape(bf16[728,728]{1,0:T(8,128)(2,1)S(1)} %convolution_convert_fusion) | data formatting | bytes 2119936
  71.5 2.4 %convert_element_type.73 = bf16[16,1,33124]{2,1,0:T(2,128)(2,1)S(1)} reshape(bf16[529984]{0:T(1024)(128)(2,1)} %reshape.172) | data formatting | bytes 2119936 | tf_op jit(solution)/shard_map/convert_element_type | solution.py:128
  74.4 8.6 %reduce.24 = bf16[16,33124]{1,0:T(8,128)(2,1)} reduce(bf16[16,1,33124]{2,1,0:T(2,128)(2,1)S(1)} %convert_element_type.73, bf16[]{:T(256)} %broadcast.99), dimensions={1}, to_apply=%convert_element_type.73.reduce_sub_computation | reduce | bytes 2119938 | tf_op jit(solution)/shard_map/convert_element_type | solution.py:128
  83.1 2.9 %reshape.174 = bf16[16,2,16562]{2,1,0:T(2,128)(2,1)} reshape(bf16[16,33124]{1,0:T(8,128)(2,1)} %reduce.24) | data formatting | bytes 2119936
  85.9 4.5 %all-to-all-start.4 = ((bf16[16,2,16562]{2,1,0:T(2,128)(2,1)}), bf16[16,2,16562]{2,1,0:T(2,128)(2,1)}, u32[]{:S(2)}, u32[]{:S(2)}) async-start(bf16[16,2,16562]{2,1,0:T(2,128)(2,1)} %reshape.174), calls=%async_computation.4 | async-start | bytes 2129920 | tf_op jit(solution)/shard_map/all_to_all | solution.py:32
  90.5 1.4 fusion.41
  91.9 21.6 %all-to-all-done.4 = bf16[16,2,16562]{2,1,0:T(2,128)(2,1)} async-done(((bf16[16,2,16562]{2,1,0:T(2,128)(2,1)}), bf16[16,2,16562]{2,1,0:T(2,128)(2,1)}, u32[]{:S(2)}, u32[]{:S(2)}) %all-to-all-start.4) | async-done | bytes 1060000 | tf_op jit(solution)/shard_map/all_to_all | solution.py:32
  113.5 5.3 %reshape.175 = bf16[16,1,33124]{2,1,0:T(2,128)(2,1)S(1)} reshape(bf16[16,2,16562]{2,1,0:T(2,128)(2,1)} %all-to-all-done.4) | data formatting | bytes 2119936
  118.8 2.7 %convert_reduce_fusion = f32[33124]{0:T(1024)S(1)} fusion(bf16[16,1,33124]{2,1,0:T(2,128)(2,1)S(1)} %reshape.175), kind=kLoop, calls=%fused_computation.16 | loop fusion | flops 1026844 | bytes 1192464 | tf_op jit(solution)/shard_map/reduce_sum | solution.py:33
  121.6 1.0 all_to_all.44
  122.6 36.6 %all-to-all-start.5 = ((f32[64,1,518]{2,1,0:T(1,128)}), f32[64,1,518]{2,1,0:T(1,128)S(1)}, u32[]{:S(2)}, u32[]{:S(2)}) async-start(f32[64,1,518]{2,1,0:T(1,128)} %all_to_all.44), calls=%async_computation.5 | async-start | bytes 327680 | tf_op jit(solution)/shard_map/all_to_all | solution.py:38
  159.2 5.7 %fusion.36 = bf16[1,16,16,728]{3,2,0,1:T(8,128)(2,1)} fusion(f32[728]{0:T(1024)S(1)} %get-tuple-element.27, f32[1,16,16,728]{3,2,1,0:T(8,128)} %bitcast.38, f32[728]{0:T(1024)S(1)} %get-tuple-element.28, f32[728]{0:T(1024)S(1)} %get-tuple-element.21, f32[728]{0:T(1024)S(1)} %get-tuple-element.22, f32[728]{0:T(1024)S(1)} %get-tuple-element.23, ...), kind=kLoop, calls=%fused_computation.62 | loop fusion | flops 4100096 | bytes 1889888 | tf_op jit(solution)/shard_map/convert_element_type | solution.py:126
  164.9 4.4 %all-to-all-done.5 = f32[64,1,518]{2,1,0:T(1,128)S(1)} async-done(((f32[64,1,518]{2,1,0:T(1,128)}), f32[64,1,518]{2,1,0:T(1,128)S(1)}, u32[]{:S(2)}, u32[]{:S(2)}) %all-to-all-start.5) | async-done | bytes 132640 | tf_op jit(solution)/shard_map/all_to_all | solution.py:38
  169.2 5.6 %all-to-all-start.3 = ((bf16[1,16,16,728]{3,2,0,1:T(8,128)(2,1)}), bf16[1,16,16,728]{3,2,0,1:T(8,128)(2,1)S(1)}, u32[]{:S(2)}, u32[]{:S(2)}) async-start(bf16[1,16,16,728]{3,2,0,1:T(8,128)(2,1)} %fusion.36), calls=%async_computation.3 | async-start | bytes 786432 | tf_op jit(solution)/shard_map/all_to_all | solution.py:127
  175.0 16.8 %all-to-all-done.3 = bf16[1,16,16,728]{3,2,0,1:T(8,128)(2,1)S(1)} async-done(((bf16[1,16,16,728]{3,2,0,1:T(8,128)(2,1)}), bf16[1,16,16,728]{3,2,0,1:T(8,128)(2,1)S(1)}, u32[]{:S(2)}, u32[]{:S(2)}) %all-to-all-start.3) | async-done | bytes 372768 | tf_op jit(solution)/shard_map/all_to_all | solution.py:127
  191.8 0.8 broadcast_in_dim.9
  192.5 8.7 %all-to-all-start.6 = ((f32[64,1,518]{2,1,0:T(1,128)}), f32[64,1,518]{2,1,0:T(1,128)S(1)}, u32[]{:S(2)}, u32[]{:S(2)}) async-start(f32[64,1,518]{2,1,0:T(1,128)} %broadcast_in_dim.9), calls=%async_computation.6 | async-start | bytes 327680 | tf_op jit(solution)/shard_map/all_to_all | solution.py:9
  201.3 0.9 copy.42
  202.2 9.2 %all-to-all-done.6 = f32[64,1,518]{2,1,0:T(1,128)S(1)} async-done(((f32[64,1,518]{2,1,0:T(1,128)}), f32[64,1,518]{2,1,0:T(1,128)S(1)}, u32[]{:S(2)}, u32[]{:S(2)}) %all-to-all-start.6) | async-done | bytes 132640 | tf_op jit(solution)/shard_map/all_to_all | solution.py:9
  211.8 0.9 reshape.160
  (42 shorter events, 5.6 us)
Async XLA Ops:
  0.6 29.1 %copy-start = (bf16[728,728]{1,0:T(8,128)(2,1)S(1)}, bf16[728,728]{1,0:T(8,128)(2,1)}, u32[]{:S(2)}) copy-start(bf16[728,728]{1,0:T(8,128)(2,1)} %param.9) | copy-start | bytes 3179908
  0.6 28.4 %all-to-all-start = ((bf16[16,1,16,728]{3,2,1,0:T(8,128)(2,1)}), bf16[16,1,16,728]{3,2,1,0:T(8,128)(2,1)S(1)}, u32[]{:S(2)}, u32[]{:S(2)}) async-start(bf16[16,1,16,728]{3,2,1,0:T(8,128)(2,1)} %param.6), calls=%async_computation | async-start | bytes 786432 | tf_op jit(solution)/shard_map/all_to_all | solution.py:80
  29.1 23.1 %copy-start.1 = (bf16[16,1,16,728]{3,2,1,0:T(8,128)(2,1)}, bf16[16,1,16,728]{3,2,1,0:T(8,128)(2,1)S(1)}, u32[]{:S(2)}) copy-start(bf16[16,1,16,728]{3,2,1,0:T(8,128)(2,1)S(1)} %all-to-all-done) | copy-start | bytes 1118212
  29.7 0.8 copy-start.5
  29.7 5.1 %copy-start.3 = (bf16[1,16,16,728]{3,2,1,0:T(8,128)(2,1)S(1)}, bf16[1,16,16,728]{3,2,1,0:T(8,128)(2,1)}, u32[]{:S(2)}) copy-start(bf16[1,16,16,728]{3,2,1,0:T(8,128)(2,1)} %param.7) | copy-start | bytes 1118212
  30.6 4.5 %copy-start.10 = (f32[728]{0:T(1024)S(1)}, f32[728]{0:T(1024)}, u32[]{:S(2)}) copy-start(f32[728]{0:T(1024)} %param.10) | copy-start | bytes 8740
  31.4 15.7 %all-to-all-start.1 = ((f32[16,1,1456]{2,1,0:T(1,128)}), f32[16,1,1456]{2,1,0:T(1,128)S(1)}, u32[]{:S(2)}, u32[]{:S(2)}) async-start(f32[16,1,1456]{2,1,0:T(1,128)} %broadcast_in_dim.7), calls=%async_computation.1 | async-start | bytes 196608 | tf_op jit(solution)/shard_map/all_to_all | solution.py:9
  48.5 15.7 %all-to-all-start.2 = ((f32[16,1,1456]{2,1,0:T(1,128)}), f32[16,1,1456]{2,1,0:T(1,128)S(1)}, u32[]{:S(2)}, u32[]{:S(2)}) async-start(f32[16,1,1456]{2,1,0:T(1,128)} %broadcast_in_dim.8), calls=%async_computation.2 | async-start | bytes 196608 | tf_op jit(solution)/shard_map/all_to_all | solution.py:9
  53.2 11.2 %copy-start.11 = (f32[728]{0:T(1024)S(1)}, f32[728]{0:T(1024)}, u32[]{:S(2)}) copy-start(f32[728]{0:T(1024)} %param.11) | copy-start | bytes 8740
  64.3 3.3 %copy-start.6 = (bf16[1,16,16,728]{3,2,1,0:T(8,128)(2,1)S(1)}, bf16[1,16,16,728]{3,2,1,0:T(8,128)(2,1)}, u32[]{:S(2)}) copy-start(bf16[1,16,16,728]{3,2,1,0:T(8,128)(2,1)} %copy-done.5) | copy-start | bytes 1118212
  66.8 0.8 copy-start.7
  85.9 4.5 %copy-start.8 = (bf16[256,728]{0,1:T(8,128)(2,1)S(1)}, bf16[256,728]{0,1:T(8,128)(2,1)}, u32[]{:S(2)}) copy-start(bf16[256,728]{0,1:T(8,128)(2,1)} %copy-done.7) | copy-start | bytes 1118212
  85.9 27.5 %all-to-all-start.4 = ((bf16[16,2,16562]{2,1,0:T(2,128)(2,1)}), bf16[16,2,16562]{2,1,0:T(2,128)(2,1)}, u32[]{:S(2)}, u32[]{:S(2)}) async-start(bf16[16,2,16562]{2,1,0:T(2,128)(2,1)} %reshape.174), calls=%async_computation.4 | async-start | bytes 2129920 | tf_op jit(solution)/shard_map/all_to_all | solution.py:32
  121.5 37.6 %copy-start.2 = (bf16[16,1,16,728]{3,2,1,0:T(8,128)(2,1)S(1)}, bf16[16,1,16,728]{3,2,1,0:T(8,128)(2,1)}, u32[]{:S(2)}) copy-start(bf16[16,1,16,728]{3,2,1,0:T(8,128)(2,1)} %copy-done.1) | copy-start | bytes 1118212
  121.5 37.6 %copy-start.4 = (bf16[1,16,16,728]{3,2,1,0:T(8,128)(2,1)S(1)}, bf16[1,16,16,728]{3,2,1,0:T(8,128)(2,1)}, u32[]{:S(2)}) copy-start(bf16[1,16,16,728]{3,2,1,0:T(8,128)(2,1)} %param.7) | copy-start | bytes 1118212
  122.6 46.7 %all-to-all-start.5 = ((f32[64,1,518]{2,1,0:T(1,128)}), f32[64,1,518]{2,1,0:T(1,128)S(1)}, u32[]{:S(2)}, u32[]{:S(2)}) async-start(f32[64,1,518]{2,1,0:T(1,128)} %all_to_all.44), calls=%async_computation.5 | async-start | bytes 327680 | tf_op jit(solution)/shard_map/all_to_all | solution.py:38
  164.9 36.4 %copy-start.9 = (bf16[256,728]{0,1:T(8,128)(2,1)S(1)}, bf16[256,728]{0,1:T(8,128)(2,1)}, u32[]{:S(2)}) copy-start(bf16[256,728]{0,1:T(8,128)(2,1)} %get-tuple-element.30) | copy-start | bytes 1118212
  169.2 22.5 %all-to-all-start.3 = ((bf16[1,16,16,728]{3,2,0,1:T(8,128)(2,1)}), bf16[1,16,16,728]{3,2,0,1:T(8,128)(2,1)S(1)}, u32[]{:S(2)}, u32[]{:S(2)}) async-start(bf16[1,16,16,728]{3,2,0,1:T(8,128)(2,1)} %fusion.36), calls=%async_computation.3 | async-start | bytes 786432 | tf_op jit(solution)/shard_map/all_to_all | solution.py:127
  192.5 18.9 %all-to-all-start.6 = ((f32[64,1,518]{2,1,0:T(1,128)}), f32[64,1,518]{2,1,0:T(1,128)S(1)}, u32[]{:S(2)}, u32[]{:S(2)}) async-start(f32[64,1,518]{2,1,0:T(1,128)} %broadcast_in_dim.9), calls=%async_computation.6 | async-start | bytes 327680 | tf_op jit(solution)/shard_map/all_to_all | solution.py:9
where the time goes:
time: 214 us; the launch traced here: 213 us
  waiting for transfers between devices  86.7 us (41%)
  starting transfers between devices  75.9 us (35%)
  local copies, waits for them, and re-layouts  24.4 us (11%)
  other arithmetic  22.7 us (11%)
  matrix products  2.74 us (1%)
    all_to_all x1, starting transfers between devices, sum_at_owner(): lax.all_to_all(in_blocks(shard, dim, devices), axis, 0, 0, tiled=True)  36.6 us
    all_to_all x3, waiting for transfers between devices, sent_to_all(): return lax.all_to_all(copies, axis, split_axis=0, concat_axis=0, tiled=True)  29.8 us
    all_to_all x1, waiting for transfers between devices, summed_on_arrival(): lax.all_to_all(parts, axis, split_axis=0, concat_axis=0, tiled=True)  21.6 us
    all_to_all x1, waiting for transfers between devices, body(): lax.all_to_all(dinput, 'sp', split_axis=1, concat_axis=0, tiled=True)  16.8 us
    all_to_all x3, starting transfers between devices, sent_to_all(): return lax.all_to_all(copies, axis, split_axis=0, concat_axis=0, tiled=True)  15.9 us
    all_to_all x1, waiting for transfers between devices, body(): lax.all_to_all(acts, 'sp', split_axis=0, concat_axis=1, tiled=True)  14.2 us
    all_to_all x1, starting transfers between devices, body(): lax.all_to_all(acts, 'sp', split_axis=0, concat_axis=1, tiled=True)  13.3 us
    unnamed x28, local copies, waits for them, and re-layouts  13.2 us
  transfers between devices with their start and end apart: 7, of which 7 were waited for; matrix products, arithmetic and copies ran while one was open for 6% of the time, Pallas kernels for 0%

commit v1 on v0

v1 whole, which is shorter than its diff:
```python
import jax
import jax.numpy as jnp
import numpy as np
from jax import lax
from jax.experimental import pallas as pl
from jax.experimental.pallas import tpu as pltpu
from jax.sharding import Mesh, PartitionSpec as P

BF = jnp.bfloat16
F32 = jnp.float32
SP = ("x", "yh")
LINE = ("yl", "z")
GRP = ("yl", "z", "core")
VMEM = pl.BlockSpec(memory_space=pltpu.VMEM)


def call(kernel, outs, name, flops, *args):
    size = sum(a.size * a.dtype.itemsize for a in args)
    size += sum(int(np.prod(o.shape)) * o.dtype.itemsize for o in outs)
    return pl.pallas_call(
        kernel,
        out_shape=outs,
        in_specs=[VMEM] * len(args),
        out_specs=[VMEM] * len(outs),
        cost_estimate=pl.CostEstimate(flops=flops, bytes_accessed=size, transcendentals=0),
        name=name,
    )(*args)


def spans(width, step):
    return [(a, min(a + step, width)) for a in range(0, width, step)]


def shifted(field):
    zero = jnp.zeros_like(field[:, :1, :])
    left = jnp.concatenate([zero, field[:, :-1, :]], axis=1)
    right = jnp.concatenate([field[:, 1:, :], zero], axis=1)
    return left, field, right


def nine_taps(field, taps, flip):
    rows = field.shape[0]
    near = shifted(field)
    out = []
    for r in range(rows):
        total = None
        for i in range(3):
            src = r + (1 - i if flip else i - 1)
            if src < 0 or src >= rows:
                continue
            for j in range(3):
                part = near[2 - j if flip else j][src] * taps[i, j : j + 1, :]
                total = part if total is None else total + part
        out.append(total)
    return out


def forward_kernel(x_ref, g_ref, k_ref, w_ref, d_ref, p_ref, s_ref):
    rows, cols, width = x_ref.shape
    for a, b in spans(width, 128):
        h = jnp.maximum(x_ref[:, :, a:b].astype(F32), 0.0)
        for r, line in enumerate(nine_taps(h, k_ref[:, :, a:b], False)):
            d_ref[r * cols : (r + 1) * cols, a:b] = line.astype(BF)
    p_ref[...] = jnp.dot(d_ref[...], w_ref[...], preferred_element_type=F32)
    for a, b in spans(width, 128):
        p = p_ref[:, a:b]
        g = g_ref[:, :, a:b].astype(F32).reshape(rows * cols, b - a)
        sums = [jnp.sum(v, axis=0, keepdims=True) for v in (p, p * p, g, g * p)]
        stats = jnp.concatenate(sums, axis=0)
        for k in range(s_ref.shape[0]):
            s_ref[k, :, a:b] = stats


def pick_kernel(d_ref, i_ref, t_ref):
    width = d_ref.shape[1]
    chan = lax.broadcasted_iota(jnp.int32, (t_ref.shape[0], width), 1)
    pick = jnp.where(chan == i_ref[...], 1.0, 0.0).astype(BF)
    t = lax.dot_general(pick, d_ref[...], (((1,), (1,)), ((), ())), preferred_element_type=F32)
    t_ref[...] = t.astype(BF)


def project_kernel(count, s_ref, p_ref, g_ref, gain_ref, t_ref, c_ref, dp_ref, o_ref):
    rows, cols, width = g_ref.shape
    for a, b in spans(width, 128):
        stats = s_ref[0, :, a:b]
        for k in range(1, s_ref.shape[0]):
            stats = stats + s_ref[k, :, a:b]
        gain = gain_ref[:, a:b]
        mean = stats[0:1] / count
        var = stats[1:2] / count - mean * mean
        rstd = lax.rsqrt(var + 1e-05)
        lead = gain * stats[2:3] / count
        second = gain * rstd * (stats[3:4] - mean * stats[2:3]) / count
        c_ref[0:1, a:b] = mean
        c_ref[1:2, a:b] = rstd
        g = g_ref[:, :, a:b].astype(F32).reshape(rows * cols, b - a)
        xhat = (p_ref[:, a:b] - mean) * rstd
        dp_ref[:, a:b] = (rstd * (g * gain - lead - xhat * second)).astype(BF)
    half = t_ref.shape[0] // 2
    other = jnp.dot(t_ref[half:, :], dp_ref[...], preferred_element_type=F32).astype(BF)
    n, part, _ = o_ref.shape
    for k in range(n):
        o_ref[k] = other[k * part : (k + 1) * part, :]


def input_kernel(dp_ref, t_ref, w_ref, k_ref, g_ref, x_ref, m_ref, di_ref, dd_ref):
    rows, cols, width = g_ref.shape
    half = t_ref.shape[0] // 2
    m_ref[...] = jnp.dot(t_ref[:half, :], dp_ref[...], preferred_element_type=F32)
    dd_ref[...] = lax.dot_general(
        dp_ref[...], w_ref[...], (((1,), (1,)), ((), ())), preferred_element_type=F32
    )
    for a, b in spans(width, 128):
        dd = dd_ref[:, a:b].reshape(rows, cols, b - a)
        for r, line in enumerate(nine_taps(dd, k_ref[:, :, a:b], True)):
            kept = jnp.where(x_ref[r, :, a:b].astype(F32) > 0, line, 0.0)
            di_ref[r, :, a:b] = (g_ref[r, :, a:b].astype(F32) + kept).astype(BF)


def output_kernel(x_ref, p_ref, c_ref, gain_ref, bias_ref, o_ref):
    rows, cols, width = x_ref.shape
    for a, b in spans(width, 128):
        xhat = (p_ref[:, a:b] - c_ref[0:1, a:b]) * c_ref[1:2, a:b]
        norm = (gain_ref[:, a:b] * xhat).reshape(rows, cols, b - a)
        out = x_ref[:, :, a:b].astype(F32) + norm + bias_ref[:, a:b]
        o_ref[:, :, a:b] = out.astype(BF)


def pack_kernel(m_ref, r_ref, di_ref, o_ref):
    n, cols, _ = di_ref.shape
    part = m_ref.shape[0] // n
    for k in range(n):
        rows = slice(k * part, (k + 1) * part)
        o_ref[k, :part, :] = (m_ref[rows, :] + r_ref[k].astype(F32)).astype(BF)
        o_ref[k, part:, :] = di_ref[k]


def slice_kernel(b_ref, o_ref):
    n = b_ref.shape[0]
    lines, per, width = o_ref.shape
    part = b_ref.shape[1] - 16
    total = b_ref[0, :part, :].astype(F32)
    for k in range(1, n):
        total = total + b_ref[k, :part, :].astype(F32)
    for k in range(lines):
        for q in range(per):
            r = k * per + q
            if r < part:
                o_ref[k, q : q + 1, :] = total[r : r + 1, :]
            else:
                o_ref[k, q : q + 1, :] = jnp.zeros((1, width), F32)


def out(shape, dtype):
    return jax.ShapeDtypeStruct(shape, dtype)


def channel_table(width, parts):
    per = -(-(width * width // parts) // width)
    half = -(-(per // 2 + 1) // 8) * 8
    table = np.full((2, parts, half), -1, np.int32)
    for c in range(2):
        for k in range(parts):
            first = (width * k) // parts
            for r in range(half):
                row = 2 * r + c
                if row < per and first + row < width:
                    table[c, k, r] = first + row
    return table.reshape(2, parts * half), half, per


def body(acts, cotangent, depth_kernel, point_weight, gain, bias):
    n = lax.axis_size(SP)
    lines = lax.axis_size(LINE)
    copies = lax.axis_size(GRP)
    _, rows, cols, width = cotangent.shape
    places = rows * cols
    count = places * n
    table, half, per = channel_table(width, n)
    core = lax.axis_index("core")
    mine = jnp.where(core == 0, table.reshape(-1), table[::-1].reshape(-1))[:, None]
    gain = gain[None]
    bias = bias[None]
    g = cotangent[0]

    x = lax.all_to_all(acts[:, 0], SP, 0, 0, tiled=True)
    d, p, stats = call(
        forward_kernel,
        [out((places, width), BF), out((places, width), F32), out((n, 4, width), F32)],
        "forward", 2 * places * width * width, x, g, depth_kernel, point_weight,
    )
    stats = lax.all_to_all(stats, SP, 0, 0, tiled=True)
    (picked,) = call(
        pick_kernel, [out((2 * n * half, places), BF)], "pick",
        4 * places * width * n * half, d, mine,
    )
    coefs, dp, other = call(
        lambda *refs: project_kernel(float(count), *refs),
        [out((2, width), F32), out((places, width), BF), out((n, half, width), BF)],
        "project", 2 * places * width * n * half, stats, p, g, gain, picked,
    )
    other = lax.ppermute(other, "core", [(0, 1), (1, 0)])
    own, dinput, _ = call(
        input_kernel,
        [out((n * half, width), F32), out((rows, cols, width), BF), out((places, width), F32)],
        "input", 4 * places * width * width, dp, picked, point_weight, depth_kernel, g, x,
    )
    (packed,) = call(
        pack_kernel, [out((n, half + cols, width), BF)], "pack", n * half * width, own, other, dinput
    )
    packed = lax.all_to_all(packed, SP, 0, 0, tiled=True)
    (block_out,) = call(
        output_kernel, [out((rows, cols, width), BF)], "output", 4 * places * width,
        x, p, coefs, gain, bias,
    )
    each = -(-half // lines)
    (pieces,) = call(
        slice_kernel, [out((lines, each, width), F32)], "slice", n * half * width, packed
    )
    pieces = lax.all_to_all(pieces, LINE, 0, 0, tiled=True)
    summed = jnp.broadcast_to(jnp.sum(pieces, axis=0), (copies, each, width))
    whole = lax.all_to_all(summed, GRP, 0, 0, tiled=True)
    whole = whole.reshape(lines, 2, each, width).swapaxes(1, 2).reshape(-1)
    span = width * width // n
    shift = (lax.axis_index(SP) * span) % width
    if (2 * span) % width == 0:
        odd = shift != 0
        weight_grad = jnp.where(odd, whole[width // 2 : width // 2 + span], whole[:span])
    else:
        weight_grad = lax.dynamic_slice(whole, (shift,), (span,))
    input_grad = packed[:, half:, :][:, None]
    return block_out[None], input_grad, weight_grad


def solution(mesh):
    sizes = (4, mesh.shape["grp"] // 8, 2, mesh.shape["sp"] // 2, 2)
    fine = Mesh(mesh.devices.reshape(sizes), ("yl", "z", "core", "x", "yh"))
    in_specs = (P(GRP, SP, None, None), P(GRP + SP, None, None, None), P(), P(), P(), P())
    out_specs = (P(GRP + SP, None, None, None), P(GRP, SP, None, None), P(SP))
    return jax.shard_map(body, mesh=fine, in_specs=in_specs, out_specs=out_specs, check_vma=False)
```

time: 214 us -> 154 us (0.72)
  blocking collectives: 0 us -> 90.1 us
  waiting for transfers between devices: 86.7 us -> 15.3 us
  starting transfers between devices: 75.9 us -> 20 us
  other arithmetic: 22.7 us -> 1.31 us
  Pallas kernels: 0 us -> 19.5 us
  local copies, waits for them, and re-layouts: 24.4 us -> 6.31 us
  matrix products: 2.74 us -> 0 us
    all_to_all x0 -> x3, blocking collectives: none -> 90.1 us  [the longest x1 34.7 us: body(): packed = lax.all_to_all(packed, SP, 0, 0, tiled=True)]
    all_to_all x7 -> x2, waiting for transfers between devices: 86.7 us -> 15.3 us  [the longest x1 9.16 us: body(): stats = lax.all_to_all(stats, SP, 0, 0, tiled=True)]
    all_to_all x7 -> x2, starting transfers between devices: 75.9 us -> 10.4 us  [the longest x1 6.91 us: body(): whole = lax.all_to_all(summed, GRP, 0, 0, tiled=True)]
    pallas_call x0 -> x7, Pallas kernels: none -> 19.5 us  [call(): pl.pallas_call(kernel, out_shape=outs, in_specs=[VMEM] * len(args), out_s...]
    convert_element_type x5 -> x0, other arithmetic: 18.4 us -> none  [the longest x1 8.65 us: body(): slices = summed_on_arrival(local_weight.astype(jnp.bfloat16), 'sp', 0)]
    unnamed x28 -> x13, local copies, waits for them, and re-layouts: 13.2 us -> 3.28 us
    ppermute x0 -> x1, starting transfers between devices: none -> 9.54 us  [body(): other = lax.ppermute(other, 'core', [(0, 1), (1, 0)])]
    convert_element_type x4 -> x0, local copies, waits for them, and re-layouts: 6.09 us -> none  [the longest x2 2.88 us: body(): slices = summed_on_arrival(local_weight.astype(jnp.bfloat16), 'sp', 0)]
  transfers between devices with their start and end apart: 7 -> 3, of which waited for: 7 -> 2; matrix products, arithmetic and copies ran while one was open for 6% -> 3% of each run, Pallas kernels for 0% -> 6%
where the time goes in v1:
time: 154 us; the launch traced here: 153 us
  blocking collectives  90.1 us (59%)
  starting transfers between devices  20 us (13%)
  Pallas kernels  19.5 us (13%)
  waiting for transfers between devices  15.3 us (10%)
  local copies, waits for them, and re-layouts  6.31 us (4%)
    all_to_all x1, blocking collectives, body(): packed = lax.all_to_all(packed, SP, 0, 0, tiled=True)  34.7 us
    all_to_all x1, blocking collectives, body(): x = lax.all_to_all(acts[:, 0], SP, 0, 0, tiled=True)  28.1 us
    all_to_all x1, blocking collectives, body(): pieces = lax.all_to_all(pieces, LINE, 0, 0, tiled=True)  27.3 us
    pallas_call x7, Pallas kernels, call(): pl.pallas_call(kernel, out_shape=outs, in_specs=[VMEM] * len(args), out_s...  19.5 us
    ppermute x1, starting transfers between devices, body(): other = lax.ppermute(other, 'core', [(0, 1), (1, 0)])  9.54 us
    all_to_all x1, waiting for transfers between devices, body(): stats = lax.all_to_all(stats, SP, 0, 0, tiled=True)  9.16 us
    all_to_all x1, starting transfers between devices, body(): whole = lax.all_to_all(summed, GRP, 0, 0, tiled=True)  6.91 us
    all_to_all x1, waiting for transfers between devices, body(): whole = lax.all_to_all(summed, GRP, 0, 0, tiled=True)  6.12 us
  transfers between devices with their start and end apart: 3, of which 2 were waited for; matrix products, arithmetic and copies ran while one was open for 3% of the time, Pallas kernels for 6%

profile of v1, /device:TPU:1, one launch (start us, length us, event | category | flops | bytes accessed | tf_op | source)
XLA Modules:
  0.0 153.2 jit_solution(14809529461273709091)
XLA Ops:
  0.6 28.1 %all_to_all.25.x_ref = bf16[16,16,728]{2,1,0:T(8,128)(2,1)} all-to-all(bf16[16,16,728]{2,1,0:T(8,128)(2,1)} %bitcast.10), channel_id=1, replica_groups=mesh['yl'=4,'z'=8,'core'=2,'x'=8,'yh'=2] {'x','yh'}, dimensions={0} | all-to-all | bytes 745472 | tf_op jit(solution)/shard_map/all_to_all | solution.py:186
  28.8 0.0 copy-start.4
  28.8 3.6 %forward.1 = (bf16[256,728]{1,0:T(8,128)(2,1)}, f32[256,728]{1,0:T(8,128)}, f32[16,4,728]{2,1,0:T(4,128)}) custom-call(bf16[16,16,728]{2,1,0:T(8,128)(2,1)} %all_to_all.25.x_ref, bf16[16,16,728]{2,1,0:T(8,128)(2,1)} %bitcast.7, f32[3,3,728]{2,1,0:T(4,128)} %k_ref.3, bf16[728,728]{1,0:T(8,128)(2,1)} %w_ref.3), custom_call_target="tpu_custom_call" | custom-call | flops 271351808 | bytes 3136224 | tf_op jit(solution)/shard_map/forward/pallas_call | solution.py:20
  32.3 3.5 %all-to-all-start.1 = ((f32[16,4,728]{2,1,0:T(4,128)}), f32[16,4,728]{2,1,0:T(4,128)S(1)}, u32[]{:S(2)}, u32[]{:S(2)}) async-start(f32[16,4,728]{2,1,0:T(4,128)} %get-tuple-element.12), calls=%async_computation.1 | async-start | bytes 393216 | tf_op jit(solution)/shard_map/all_to_all | solution.py:192
  35.9 0.0 copy-done.4
  35.9 0.6 broadcast_in_dim.18.refs_3_.gain_ref
  36.5 0.0 copy-done.2
  36.5 0.0 copy-done.3
  36.5 0.9 broadcast_in_dim.24.i_ref
  37.4 2.5 %pick.1.refs_4_.t_ref = bf16[768,256]{1,0:T(8,128)(2,1)} custom-call(bf16[256,728]{1,0:T(8,128)(2,1)} %get-tuple-element.13.d_ref, s32[768,1]{1,0:T(8,128)} %broadcast_in_dim.24.i_ref), custom_call_target="tpu_custom_call" | custom-call | flops 286261248 | bytes 769024 | tf_op jit(solution)/shard_map/pick/pallas_call | solution.py:20
  39.8 9.2 %all-to-all-done.1.refs_0_ = f32[16,4,728]{2,1,0:T(4,128)S(1)} async-done(((f32[16,4,728]{2,1,0:T(4,128)}), f32[16,4,728]{2,1,0:T(4,128)S(1)}, u32[]{:S(2)}, u32[]{:S(2)}) %all-to-all-start.1) | async-done | bytes 186400 | tf_op jit(solution)/shard_map/all_to_all | solution.py:192
  49.0 0.7 copy-done
  49.7 2.9 %project.1 = (f32[2,728]{1,0:T(2,128)}, bf16[256,728]{1,0:T(8,128)(2,1)}, bf16[16,24,728]{2,1,0:T(8,128)(2,1)}) custom-call(f32[16,4,728]{2,1,0:T(4,128)} %copy-done, f32[256,728]{1,0:T(8,128)} %get-tuple-element.11.refs_1_.p_ref, bf16[16,16,728]{2,1,0:T(8,128)(2,1)} %bitcast.8, f32[1,728]{1,0:T(1,128)} %broadcast_in_dim.18.refs_3_.gain_ref, ...), custom_call_target="tpu_custom_call" | custom-call | flops 143130624 | bytes 2638368 | tf_op jit(solution)/shard_map/project/pallas_call | solution.py:20
  52.6 9.5 %collective-permute-start = (bf16[16,24,728]{2,1,0:T(8,128)(2,1)}, bf16[16,24,728]{2,1,0:T(8,128)(2,1)S(1)}, u32[]{:S(2)}, u32[]{:S(2)}) collective-permute-start(bf16[16,24,728]{2,1,0:T(8,128)(2,1)} %get-tuple-element.17), channel_id=1, source_target_pairs={{0,16},{16,0},{1,17},{17,1},{2,18},{18,2},{3,19},{19,3},{4,20},{20... | collective-permute-start | bytes 1677320 | tf_op jit(solution)/shard_map/ppermute | solution.py:202
  62.1 3.9 %input.1 = (f32[384,728]{1,0:T(8,128)}, bf16[16,16,728]{2,1,0:T(8,128)(2,1)}, f32[256,728]{1,0:T(8,128)}) custom-call(bf16[256,728]{1,0:T(8,128)(2,1)} %get-tuple-element.15.dp_ref, bf16[768,256]{1,0:T(8,128)(2,1)} %pick.1.refs_4_.t_ref, bf16[728,728]{1,0:T(8,128)(2,1)} %w_ref.3, f32[3,3,728]{2,1,0:T(4,128)} %k_ref.3, bf16[16,16,728]{2,1,0:T(8,128)(2,1)} %bitcast.9, ...), custom_call_target="tpu_custom_call" | custom-call | flops 542703616 | bytes 4834016 | tf_op jit(solution)/shard_map/input/pallas_call | solution.py:20
  66.0 0.0 collective-permute-done.r_ref
  66.0 0.8 copy-done.1
  66.8 2.6 %pack.1 = bf16[16,40,728]{2,1,0:T(8,128)(2,1)} custom-call(f32[384,728]{1,0:T(8,128)} %get-tuple-element.16.m_ref, bf16[16,24,728]{2,1,0:T(8,128)(2,1)} %copy-done.1, bf16[16,16,728]{2,1,0:T(8,128)(2,1)} %get-tuple-element.18.di_ref), custom_call_target="tpu_custom_call" | custom-call | flops 279552 | bytes 2981888 | tf_op jit(solution)/shard_map/pack/pallas_call | solution.py:20
  69.4 34.7 %all_to_all.26.b_ref = bf16[16,40,728]{2,1,0:T(8,128)(2,1)} all-to-all(bf16[16,40,728]{2,1,0:T(8,128)(2,1)} %pack.1), channel_id=1, replica_groups=mesh['yl'=4,'z'=8,'core'=2,'x'=8,'yh'=2] {'x','yh'}, dimensions={0} | all-to-all | bytes 1863680 | tf_op jit(solution)/shard_map/all_to_all | solution.py:211
  104.1 1.9 %slice.19 = f32[32,1,728]{2,1,0:T(1,128)} custom-call(bf16[16,40,728]{2,1,0:T(8,128)(2,1)} %all_to_all.26.b_ref), custom_call_target="tpu_custom_call" | custom-call | flops 279552 | bytes 1025024 | tf_op jit(solution)/shard_map/slice/pallas_call | solution.py:20
  106.0 27.3 %all_to_all.27 = f32[32,1,728]{2,1,0:T(1,128)S(1)} all-to-all(f32[32,1,728]{2,1,0:T(1,128)} %slice.19), channel_id=1, replica_groups=mesh['yl'=4,'z'=8,'core'=2,'x'=8,'yh'=2] {'yl','z'}, dimensions={0} | all-to-all | bytes 186368 | tf_op jit(solution)/shard_map/all_to_all | solution.py:220
  133.3 0.1 reduce_sum.9
  133.4 0.8 broadcast_in_dim.23
  134.2 6.9 %all-to-all-start.4 = ((f32[64,1,728]{2,1,0:T(1,128)}), f32[64,1,728]{2,1,0:T(1,128)S(1)}, u32[]{:S(2)}, u32[]{:S(2)}) async-start(f32[64,1,728]{2,1,0:T(1,128)} %broadcast_in_dim.23), calls=%async_computation.4 | async-start | bytes 393216 | tf_op jit(solution)/shard_map/all_to_all | solution.py:222
  141.1 0.0 copy-done.5
  141.1 0.6 broadcast_in_dim.20.bias_ref
  141.7 2.2 %output.1 = bf16[16,16,728]{2,1,0:T(8,128)(2,1)} custom-call(bf16[16,16,728]{2,1,0:T(8,128)(2,1)} %all_to_all.25.x_ref, f32[256,728]{1,0:T(8,128)} %get-tuple-element.11.refs_1_.p_ref, f32[2,728]{1,0:T(2,128)} %get-tuple-element.14.c_ref, f32[1,728]{1,0:T(1,128)} %broadcast_in_dim.18.refs_3_.gain_ref, f32[1,728]{1,0:T(1,128)} %broadcast_in_dim.20.bias_ref), custom_call_target="tpu_custom_call" | custom-call | flops 745472 | bytes 1502592 | tf_op jit(solution)/shard_map/output/pallas_call | solution.py:20
  143.9 1.8 %slice_bitcast_fusion = bf16[16,1,16,728]{3,2,1,0:T(8,128)(2,1)} fusion(bf16[16,40,728]{2,1,0:T(8,128)(2,1)} %all_to_all.26.b_ref), kind=kLoop, calls=%fused_computation | loop fusion | bytes 745472
  145.6 6.1 %all-to-all-done.4 = f32[64,1,728]{2,1,0:T(1,128)S(1)} async-done(((f32[64,1,728]{2,1,0:T(1,128)}), f32[64,1,728]{2,1,0:T(1,128)S(1)}, u32[]{:S(2)}, u32[]{:S(2)}) %all-to-all-start.4) | async-done | bytes 186400 | tf_op jit(solution)/shard_map/all_to_all | solution.py:222
  151.8 0.5 reduce.1
  152.2 0.2 reshape_transpose_reshape.3
  152.4 0.8 slice_select_fusion
  (6 shorter events, 0.0 us)
Async XLA Ops:
  28.8 7.1 %copy-start.4 = (f32[728]{0:T(1024)S(1)}, f32[728]{0:T(1024)}, u32[]{:S(2)}) copy-start(f32[728]{0:T(1024)} %param.12) | copy-start | bytes 8740
  28.8 7.7 %copy-start.2 = (s32[768]{0:T(1024)S(1)}, s32[768]{0:T(1024)}, u32[]{:S(2)}) copy-start(s32[768]{0:T(1024)} %constant.34.clone) | copy-start | bytes 9220
  28.8 7.7 %copy-start.3 = (s32[768]{0:T(1024)S(1)}, s32[768]{0:T(1024)}, u32[]{:S(2)}) copy-start(s32[768]{0:T(1024)} %constant.33.clone) | copy-start | bytes 9220
  32.3 16.7 %all-to-all-start.1 = ((f32[16,4,728]{2,1,0:T(4,128)}), f32[16,4,728]{2,1,0:T(4,128)S(1)}, u32[]{:S(2)}, u32[]{:S(2)}) async-start(f32[16,4,728]{2,1,0:T(4,128)} %get-tuple-element.12), calls=%async_computation.1 | async-start | bytes 393216 | tf_op jit(solution)/shard_map/all_to_all | solution.py:192
  49.0 0.7 copy-start
  52.6 13.4 %collective-permute-start = (bf16[16,24,728]{2,1,0:T(8,128)(2,1)}, bf16[16,24,728]{2,1,0:T(8,128)(2,1)S(1)}, u32[]{:S(2)}, u32[]{:S(2)}) collective-permute-start(bf16[16,24,728]{2,1,0:T(8,128)(2,1)} %get-tuple-element.17), channel_id=1, source_target_pairs={{0,16},{16,0},{1,17},{17,1},{2,18},{18,2},{3,19},{19,3},{4,20},{20... | collective-permute-start | bytes 1677320 | tf_op jit(solution)/shard_map/ppermute | solution.py:202
  66.0 0.8 copy-start.1
  104.1 37.0 %copy-start.5 = (f32[728]{0:T(1024)S(1)}, f32[728]{0:T(1024)}, u32[]{:S(2)}) copy-start(f32[728]{0:T(1024)} %param.13) | copy-start | bytes 8740
  134.2 17.6 %all-to-all-start.4 = ((f32[64,1,728]{2,1,0:T(1,128)}), f32[64,1,728]{2,1,0:T(1,128)S(1)}, u32[]{:S(2)}, u32[]{:S(2)}) async-start(f32[64,1,728]{2,1,0:T(1,128)} %broadcast_in_dim.23), calls=%async_computation.4 | async-start | bytes 393216 | tf_op jit(solution)/shard_map/all_to_all | solution.py:222

commit v2 on v1

--- a/solution.py
+++ b/solution.py
@@ -14,7 +14,11 @@
 VMEM = pl.BlockSpec(memory_space=pltpu.VMEM)
 
 
-def call(kernel, outs, name, flops, *args):
+def held_in(a, space):
+    return pltpu.with_memory_space_constraint(a, space)
+
+
+def call(kernel, outs, name, flops, *args, far=()):
     size = sum(a.size * a.dtype.itemsize for a in args)
     size += sum(int(np.prod(o.shape)) * o.dtype.itemsize for o in outs)
     return pl.pallas_call(
@@ -23,8 +27,9 @@
         in_specs=[VMEM] * len(args),
         out_specs=[VMEM] * len(outs),
         cost_estimate=pl.CostEstimate(flops=flops, bytes_accessed=size, transcendentals=0),
+        compiler_params=pltpu.CompilerParams(vmem_limit_bytes=16 * 2**20),
         name=name,
-    )(*args)
+    )(*[held_in(a, pltpu.HBM if k in far else pltpu.VMEM) for k, a in enumerate(args)])
 
 
 def spans(width, step):
@@ -55,6 +60,12 @@
     return out
 
 
+def stage_kernel(*refs):
+    half = len(refs) // 2
+    for src, dst in zip(refs[:half], refs[half:]):
+        dst[...] = src[...]
+
+
 def forward_kernel(x_ref, g_ref, k_ref, w_ref, d_ref, p_ref, s_ref):
     rows, cols, width = x_ref.shape
     for a, b in spans(width, 128):
@@ -71,10 +82,21 @@
             s_ref[k, :, a:b] = stats
 
 
-def pick_kernel(d_ref, i_ref, t_ref):
+def pick_kernel(parts, d_ref, t_ref):
     width = d_ref.shape[1]
-    chan = lax.broadcasted_iota(jnp.int32, (t_ref.shape[0], width), 1)
-    pick = jnp.where(chan == i_ref[...], 1.0, 0.0).astype(BF)
+    lines = t_ref.shape[0]
+    part = lines // 2 // parts
+    per = -(-width // parts)
+    core = lax.axis_index("core")
+    line = lax.broadcasted_iota(jnp.int32, (lines, 1), 0)
+    other = line >= lines // 2
+    line = jnp.where(other, line - lines // 2, line)
+    slot = (line * (65536 // part + 1)) >> 16
+    row = 2 * (line - part * slot) + jnp.where(other, 1 - core, core)
+    source = ((slot * (2 * width // parts)) >> 1) + row
+    source = jnp.where(row < per, source, -1)
+    chan = lax.broadcasted_iota(jnp.int32, (lines, width), 1)
+    pick = jnp.where(chan == source, 1.0, 0.0).astype(BF)
     t = lax.dot_general(pick, d_ref[...], (((1,), (1,)), ((), ())), preferred_element_type=F32)
     t_ref[...] = t.astype(BF)
 
@@ -151,22 +173,16 @@
                 o_ref[k, q : q + 1, :] = jnp.zeros((1, width), F32)
 
 
+def copies_kernel(b_ref, o_ref):
+    total = b_ref[0]
+    for k in range(1, b_ref.shape[0]):
+        total = total + b_ref[k]
+    for k in range(o_ref.shape[0]):
+        o_ref[k] = total
+
+
 def out(shape, dtype):
-    return jax.ShapeDtypeStruct(shape, dtype)
-
-
-def channel_table(width, parts):
-    per = -(-(width * width // parts) // width)
-    half = -(-(per // 2 + 1) // 8) * 8
-    table = np.full((2, parts, half), -1, np.int32)
-    for c in range(2):
-        for k in range(parts):
-            first = (width * k) // parts
-            for r in range(half):
-                row = 2 * r + c
-                if row < per and first + row < width:
-                    table[c, k, r] = first + row
-    return table.reshape(2, parts * half), half, per
+    return pltpu.VMEM(shape, dtype)
 
 
 def body(acts, cotangent, depth_kernel, point_weight, gain, bias):
@@ -176,23 +192,23 @@
     _, rows, cols, width = cotangent.shape
     places = rows * cols
     count = places * n
-    table, half, per = channel_table(width, n)
-    core = lax.axis_index("core")
-    mine = jnp.where(core == 0, table.reshape(-1), table[::-1].reshape(-1))[:, None]
-    gain = gain[None]
-    bias = bias[None]
+    half = -(-(-(-width // n) // 2) // 8) * 8
     g = cotangent[0]
 
+    held = (g, depth_kernel, point_weight, gain[None], bias[None])
+    near_g, near_k, near_w, gain, bias = call(
+        stage_kernel, [out(a.shape, a.dtype) for a in held], "stage", 4 * width * width * 8, *held
+    )
     x = lax.all_to_all(acts[:, 0], SP, 0, 0, tiled=True)
     d, p, stats = call(
         forward_kernel,
-        [out((places, width), BF), out((places, width), F32), out((n, 4, width), F32)],
-        "forward", 2 * places * width * width, x, g, depth_kernel, point_weight,
+        [pltpu.HBM((places, width), BF), out((places, width), F32), out((n, 4, width), F32)],
+        "forward", 2 * places * width * width, x, near_g, near_k, near_w,
     )
     stats = lax.all_to_all(stats, SP, 0, 0, tiled=True)
     (picked,) = call(
-        pick_kernel, [out((2 * n * half, places), BF)], "pick",
-        4 * places * width * n * half, d, mine,
+        lambda *refs: pick_kernel(n, *refs), [out((2 * n * half, places), BF)], "pick",
+        4 * places * width * n * half, d, far=(0,),
     )
     coefs, dp, other = call(
         lambda *refs: project_kernel(float(count), *refs),
@@ -203,7 +219,7 @@
     own, dinput, _ = call(
         input_kernel,
         [out((n * half, width), F32), out((rows, cols, width), BF), out((places, width), F32)],
-        "input", 4 * places * width * width, dp, picked, point_weight, depth_kernel, g, x,
+        "input", 4 * places * width * width, dp, picked, point_weight, depth_kernel, g, x, far=(2,),
     )
     (packed,) = call(
         pack_kernel, [out((n, half + cols, width), BF)], "pack", n * half * width, own, other, dinput
@@ -218,7 +234,9 @@
         slice_kernel, [out((lines, each, width), F32)], "slice", n * half * width, packed
     )
     pieces = lax.all_to_all(pieces, LINE, 0, 0, tiled=True)
-    summed = jnp.broadcast_to(jnp.sum(pieces, axis=0), (copies, each, width))
+    (summed,) = call(
+        copies_kernel, [out((copies, each, width), F32)], "copies", width * width, pieces
+    )
     whole = lax.all_to_all(summed, GRP, 0, 0, tiled=True)
     whole = whole.reshape(lines, 2, each, width).swapaxes(1, 2).reshape(-1)
     span = width * width // n

time: 154 us -> 142 us (0.922)
  blocking collectives: 90.1 us -> 60.2 us
  waiting for transfers between devices: 15.3 us -> 31.2 us
  starting transfers between devices: 20 us -> 32.9 us
  Pallas kernels: 19.5 us -> 8.5 us
    all_to_all x1 -> x0, blocking collectives: 28.1 us -> none  [body(): x = lax.all_to_all(acts[:, 0], SP, 0, 0, tiled=True)]
    all_to_all x0 -> x1, starting transfers between devices: none -> 13.1 us  [body(): x = lax.all_to_all(acts[:, 0], SP, 0, 0, tiled=True)]
    pallas_call x7 -> x9, Pallas kernels: 19.5 us -> 8.5 us  [call(): pl.pallas_call(kernel, out_shape=outs, in_specs=[VMEM] * len(args), out_s...]
    all_to_all x0 -> x1, waiting for transfers between devices: none -> 10.7 us  [body(): x = lax.all_to_all(acts[:, 0], SP, 0, 0, tiled=True)]
    all_to_all x1, waiting for transfers between devices: 6.12 us -> 8.92 us  [body(): whole = lax.all_to_all(summed, GRP, 0, 0, tiled=True)]
    all_to_all x1, waiting for transfers between devices: 9.16 us -> 11.6 us  [body(): stats = lax.all_to_all(stats, SP, 0, 0, tiled=True)]
    all_to_all x1, blocking collectives: 34.7 us -> 33 us  [body(): packed = lax.all_to_all(packed, SP, 0, 0, tiled=True)]
    unnamed x13 -> x12, local copies, waits for them, and re-layouts: 3.28 us -> 4.54 us
  transfers between devices with their start and end apart: 3 -> 4, of which waited for: 2 -> 3; matrix products, arithmetic and copies ran while one was open for 3% -> 2% of each run, Pallas kernels for 6% -> 4%
where the time goes in v2:
time: 142 us; the launch traced here: 141 us
  blocking collectives  60.2 us (42%)
  starting transfers between devices  32.9 us (23%)
  waiting for transfers between devices  31.2 us (22%)
  Pallas kernels  8.5 us (6%)
  local copies, waits for them, and re-layouts  6.08 us (4%)
    all_to_all x1, blocking collectives, body(): packed = lax.all_to_all(packed, SP, 0, 0, tiled=True)  33 us
    all_to_all x1, blocking collectives, body(): pieces = lax.all_to_all(pieces, LINE, 0, 0, tiled=True)  27.2 us
    all_to_all x1, starting transfers between devices, body(): x = lax.all_to_all(acts[:, 0], SP, 0, 0, tiled=True)  13.1 us
    all_to_all x1, waiting for transfers between devices, body(): stats = lax.all_to_all(stats, SP, 0, 0, tiled=True)  11.6 us
    all_to_all x1, waiting for transfers between devices, body(): x = lax.all_to_all(acts[:, 0], SP, 0, 0, tiled=True)  10.7 us
    all_to_all x1, waiting for transfers between devices, body(): whole = lax.all_to_all(summed, GRP, 0, 0, tiled=True)  8.92 us
    ppermute x1, starting transfers between devices, body(): other = lax.ppermute(other, 'core', [(0, 1), (1, 0)])  8.71 us
    pallas_call x9, Pallas kernels, call(): pl.pallas_call(kernel, out_shape=outs, in_specs=[VMEM] * len(args), out_s...  8.5 us
  transfers between devices with their start and end apart: 4, of which 3 were waited for; matrix products, arithmetic and copies ran while one was open for 2% of the time, Pallas kernels for 4%

profile of v2, /device:TPU:1, one launch (start us, length us, event | category | flops | bytes accessed | tf_op | source)
XLA Modules:
  0.0 140.8 jit_solution(285127902669693881)
XLA Ops:
  0.6 13.1 %all-to-all-start = ((bf16[16,16,728]{2,1,0:T(8,128)(2,1)}), bf16[16,16,728]{2,1,0:T(8,128)(2,1)S(1)}, u32[]{:S(2)}, u32[]{:S(2)}) async-start(bf16[16,16,728]{2,1,0:T(8,128)(2,1)} %bitcast.11), calls=%async_computation | async-start | bytes 786432 | tf_op jit(solution)/shard_map/all_to_all | solution.py:202
  13.8 0.7 broadcast_in_dim.12.refs_3_
  14.5 0.7 broadcast_in_dim.13.refs_4_
  15.2 1.2 copy-done
  16.4 1.0 copy-done.1
  17.4 0.8 copy-done.3
  18.2 0.1 stage.1
  18.3 10.7 %all-to-all-done.x_ref = bf16[16,16,728]{2,1,0:T(8,128)(2,1)S(1)} async-done(((bf16[16,16,728]{2,1,0:T(8,128)(2,1)}), bf16[16,16,728]{2,1,0:T(8,128)(2,1)S(1)}, u32[]{:S(2)}, u32[]{:S(2)}) %all-to-all-start) | async-done | bytes 372768 | tf_op jit(solution)/shard_map/all_to_all | solution.py:202
  28.9 1.8 %forward.1 = (bf16[256,728]{1,0:T(8,128)(2,1)}, f32[256,728]{1,0:T(8,128)S(1)}, f32[16,4,728]{2,1,0:T(4,128)}) custom-call(bf16[16,16,728]{2,1,0:T(8,128)(2,1)S(1)} %all-to-all-done.x_ref, bf16[16,16,728]{2,1,0:T(8,128)(2,1)S(1)} %get-tuple-element.16.g_ref, f32[3,3,728]{2,1,0:T(4,128)S(1)} %get-tuple-element.17.k_ref, ...), custom_call_target="tpu_custom_call" | custom-call | flops 271351808 | bytes 3136224 | tf_op jit(solution)/shard_map/forward/pallas_call | solution.py:24
  30.8 3.7 %all-to-all-start.1 = ((f32[16,4,728]{2,1,0:T(4,128)}), f32[16,4,728]{2,1,0:T(4,128)S(1)}, u32[]{:S(2)}, u32[]{:S(2)}) async-start(f32[16,4,728]{2,1,0:T(4,128)} %get-tuple-element.20), calls=%async_computation.1 | async-start | bytes 393216 | tf_op jit(solution)/shard_map/all_to_all | solution.py:208
  34.4 1.5 %pick.1.refs_4_.t_ref = bf16[768,256]{1,0:T(8,128)(2,1)S(1)} custom-call(bf16[256,728]{1,0:T(8,128)(2,1)} %get-tuple-element.22.refs_0_), custom_call_target="tpu_custom_call" | custom-call | flops 286261248 | bytes 765952 | tf_op jit(solution)/shard_map/pick/pallas_call | solution.py:24
  36.0 0.0 copy-start.4
  36.0 11.6 %all-to-all-done.1.refs_0_ = f32[16,4,728]{2,1,0:T(4,128)S(1)} async-done(((f32[16,4,728]{2,1,0:T(4,128)}), f32[16,4,728]{2,1,0:T(4,128)S(1)}, u32[]{:S(2)}, u32[]{:S(2)}) %all-to-all-start.1) | async-done | bytes 186400 | tf_op jit(solution)/shard_map/all_to_all | solution.py:208
  47.6 0.0 copy-done.2
  47.6 0.6 project.1
  48.2 8.7 %collective-permute-start = (bf16[16,24,728]{2,1,0:T(8,128)(2,1)S(1)}, bf16[16,24,728]{2,1,0:T(8,128)(2,1)S(1)}, u32[]{:S(2)}, u32[]{:S(2)}) collective-permute-start(bf16[16,24,728]{2,1,0:T(8,128)(2,1)S(1)} %get-tuple-element.27), channel_id=1, source_target_pairs={{0,16},{16,0},{1,17},{17,1},{2,18},{18,2},{3,19},{19,3},{4,20},{20... | collective-permute-start | bytes 1677320 | tf_op jit(solution)/shard_map/ppermute | solution.py:218
  56.9 0.0 copy-done.4
  56.9 3.3 %input.1 = (f32[384,728]{1,0:T(8,128)S(1)}, bf16[16,16,728]{2,1,0:T(8,128)(2,1)S(1)}, f32[256,728]{1,0:T(8,128)}) custom-call(bf16[256,728]{1,0:T(8,128)(2,1)S(1)} %get-tuple-element.25.dp_ref, bf16[768,256]{1,0:T(8,128)(2,1)S(1)} %pick.1.refs_4_.t_ref, bf16[728,728]{1,0:T(8,128)(2,1)} %w_ref.1, f32[3,3,728]{2,1,0:T(4,128)S(1)} %copy-done.4, ...), custom_call_target="tpu_custom_call" | custom-call | flops 542703616 | bytes 4834016 | tf_op jit(solution)/shard_map/input/pallas_call | solution.py:24
  60.2 0.0 collective-permute-done.r_ref
  60.2 0.1 pack.1
  60.3 33.0 %all_to_all.25.b_ref = bf16[16,40,728]{2,1,0:T(8,128)(2,1)S(1)} all-to-all(bf16[16,40,728]{2,1,0:T(8,128)(2,1)S(1)} %pack.1), channel_id=1, replica_groups=mesh['yl'=4,'z'=8,'core'=2,'x'=8,'yh'=2] {'x','yh'}, dimensions={0} | all-to-all | bytes 1863680 | tf_op jit(solution)/shard_map/all_to_all | solution.py:227
  93.3 0.1 slice.19
  93.4 27.2 %all_to_all.26.b_ref = f32[32,1,728]{2,1,0:T(1,128)S(1)} all-to-all(f32[32,1,728]{2,1,0:T(1,128)S(1)} %slice.19), channel_id=1, replica_groups=mesh['yl'=4,'z'=8,'core'=2,'x'=8,'yh'=2] {'yl','z'}, dimensions={0} | all-to-all | bytes 186368 | tf_op jit(solution)/shard_map/all_to_all | solution.py:236
  120.6 0.7 copies.1
  121.3 7.4 %all-to-all-start.4 = ((f32[64,1,728]{2,1,0:T(1,128)}), f32[64,1,728]{2,1,0:T(1,128)S(1)}, u32[]{:S(2)}, u32[]{:S(2)}) async-start(f32[64,1,728]{2,1,0:T(1,128)} %copies.1), calls=%async_computation.4 | async-start | bytes 393216 | tf_op jit(solution)/shard_map/all_to_all | solution.py:240
  128.7 0.2 output.1
  128.9 0.7 copy.10
  129.7 0.8 slice_bitcast_fusion
  130.5 8.9 %all-to-all-done.4 = f32[64,1,728]{2,1,0:T(1,128)S(1)} async-done(((f32[64,1,728]{2,1,0:T(1,128)}), f32[64,1,728]{2,1,0:T(1,128)S(1)}, u32[]{:S(2)}, u32[]{:S(2)}) %all-to-all-start.4) | async-done | bytes 186400 | tf_op jit(solution)/shard_map/all_to_all | solution.py:240
  139.4 0.5 reduce
  139.9 0.2 reshape_transpose_reshape.3
  140.0 0.8 slice_select_fusion
  (4 shorter events, 0.0 us)
Async XLA Ops:
  0.6 28.3 %all-to-all-start = ((bf16[16,16,728]{2,1,0:T(8,128)(2,1)}), bf16[16,16,728]{2,1,0:T(8,128)(2,1)S(1)}, u32[]{:S(2)}, u32[]{:S(2)}) async-start(bf16[16,16,728]{2,1,0:T(8,128)(2,1)} %bitcast.11), calls=%async_computation | async-start | bytes 786432 | tf_op jit(solution)/shard_map/all_to_all | solution.py:202
  15.1 1.2 copy-start
  16.4 1.0 copy-start.1
  17.4 0.8 copy-start.3
  30.8 16.8 %copy-start.2 = (bf16[1,16,16,728]{3,2,1,0:T(8,128)(2,1)S(1)}, bf16[1,16,16,728]{3,2,1,0:T(8,128)(2,1)}, u32[]{:S(2)}) copy-start(bf16[1,16,16,728]{3,2,1,0:T(8,128)(2,1)} %param.7) | copy-start | bytes 1118212
  30.8 16.8 %all-to-all-start.1 = ((f32[16,4,728]{2,1,0:T(4,128)}), f32[16,4,728]{2,1,0:T(4,128)S(1)}, u32[]{:S(2)}, u32[]{:S(2)}) async-start(f32[16,4,728]{2,1,0:T(4,128)} %get-tuple-element.20), calls=%async_computation.1 | async-start | bytes 393216 | tf_op jit(solution)/shard_map/all_to_all | solution.py:208
  36.0 20.9 %copy-start.4 = (f32[3,3,728]{2,1,0:T(4,128)S(1)}, f32[3,3,728]{2,1,0:T(4,128)}, u32[]{:S(2)}) copy-start(f32[3,3,728]{2,1,0:T(4,128)} %k_ref.1) | copy-start | bytes 78628
  48.2 12.0 %collective-permute-start = (bf16[16,24,728]{2,1,0:T(8,128)(2,1)S(1)}, bf16[16,24,728]{2,1,0:T(8,128)(2,1)S(1)}, u32[]{:S(2)}, u32[]{:S(2)}) collective-permute-start(bf16[16,24,728]{2,1,0:T(8,128)(2,1)S(1)} %get-tuple-element.27), channel_id=1, source_target_pairs={{0,16},{16,0},{1,17},{17,1},{2,18},{18,2},{3,19},{19,3},{4,20},{20... | collective-permute-start | bytes 1677320 | tf_op jit(solution)/shard_map/ppermute | solution.py:218
  121.3 18.0 %all-to-all-start.4 = ((f32[64,1,728]{2,1,0:T(1,128)}), f32[64,1,728]{2,1,0:T(1,128)S(1)}, u32[]{:S(2)}, u32[]{:S(2)}) async-start(f32[64,1,728]{2,1,0:T(1,128)} %copies.1), calls=%async_computation.4 | async-start | bytes 393216 | tf_op jit(solution)/shard_map/all_to_all | solution.py:240

commit v3 on v2

--- a/solution.py
+++ b/solution.py
@@ -18,7 +18,7 @@
     return pltpu.with_memory_space_constraint(a, space)
 
 
-def call(kernel, outs, name, flops, *args, far=()):
+def call(kernel, outs, flops, *args, far=()):
     size = sum(a.size * a.dtype.itemsize for a in args)
     size += sum(int(np.prod(o.shape)) * o.dtype.itemsize for o in outs)
     return pl.pallas_call(
@@ -28,7 +28,6 @@
         out_specs=[VMEM] * len(outs),
         cost_estimate=pl.CostEstimate(flops=flops, bytes_accessed=size, transcendentals=0),
         compiler_params=pltpu.CompilerParams(vmem_limit_bytes=16 * 2**20),
-        name=name,
     )(*[held_in(a, pltpu.HBM if k in far else pltpu.VMEM) for k, a in enumerate(args)])
 
 
@@ -125,18 +124,49 @@
         o_ref[k] = other[k * part : (k + 1) * part, :]
 
 
-def input_kernel(dp_ref, t_ref, w_ref, k_ref, g_ref, x_ref, m_ref, di_ref, dd_ref):
-    rows, cols, width = g_ref.shape
+def own_kernel(dp_ref, t_ref, m_ref):
     half = t_ref.shape[0] // 2
     m_ref[...] = jnp.dot(t_ref[:half, :], dp_ref[...], preferred_element_type=F32)
+
+
+def input_kernel(dp_ref, w_ref, k_ref, g_ref, x_ref, keep_ref, send_ref, dd_ref):
+    rows, cols, width = g_ref.shape
+    low = lax.axis_index("yh") == 0
     dd_ref[...] = lax.dot_general(
         dp_ref[...], w_ref[...], (((1,), (1,)), ((), ())), preferred_element_type=F32
     )
     for a, b in spans(width, 128):
         dd = dd_ref[:, a:b].reshape(rows, cols, b - a)
+        lines = []
         for r, line in enumerate(nine_taps(dd, k_ref[:, :, a:b], True)):
             kept = jnp.where(x_ref[r, :, a:b].astype(F32) > 0, line, 0.0)
-            di_ref[r, :, a:b] = (g_ref[r, :, a:b].astype(F32) + kept).astype(BF)
+            lines.append(g_ref[r, :, a:b].astype(F32) + kept)
+        for r in range(rows // 2):
+            even, odd = lines[2 * r], lines[2 * r + 1]
+            keep_ref[r, :, a:b] = jnp.where(low, even, odd).astype(BF)
+            send_ref[r, :, a:b] = jnp.where(low, odd, even).astype(BF)
+
+
+def turn_kernel(keep_ref, got_ref, *out_refs):
+    n = len(out_refs)
+    me = lax.axis_index("x")
+    low = lax.axis_index("yh") == 0
+    for k, ref in enumerate(out_refs):
+        to = lax.rem(me + k, n)
+        keep = keep_ref[to].astype(F32)
+        got = got_ref[to].astype(F32)
+        ref[0] = jnp.where(low, keep, got).astype(BF)
+        ref[1] = jnp.where(low, got, keep).astype(BF)
+
+
+def place_kernel(*refs):
+    o_ref = refs[-1]
+    n = len(refs) - 1
+    me = lax.axis_index("x")
+    for k, ref in enumerate(refs[:-1]):
+        at = 2 * lax.rem(me + n - k, n)
+        o_ref[at] = ref[0]
+        o_ref[at + 1] = ref[1]
 
 
 def output_kernel(x_ref, p_ref, c_ref, gain_ref, bias_ref, o_ref):
@@ -148,19 +178,17 @@
         o_ref[:, :, a:b] = out.astype(BF)
 
 
-def pack_kernel(m_ref, r_ref, di_ref, o_ref):
-    n, cols, _ = di_ref.shape
-    part = m_ref.shape[0] // n
+def pack_kernel(m_ref, r_ref, o_ref):
+    n, part, _ = o_ref.shape
     for k in range(n):
         rows = slice(k * part, (k + 1) * part)
-        o_ref[k, :part, :] = (m_ref[rows, :] + r_ref[k].astype(F32)).astype(BF)
-        o_ref[k, part:, :] = di_ref[k]
+        o_ref[k] = (m_ref[rows, :] + r_ref[k].astype(F32)).astype(BF)
 
 
 def slice_kernel(b_ref, o_ref):
     n = b_ref.shape[0]
     lines, per, width = o_ref.shape
-    part = b_ref.shape[1] - 16
+    part = b_ref.shape[1]
     total = b_ref[0, :part, :].astype(F32)
     for k in range(1, n):
         total = total + b_ref[k, :part, :].astype(F32)
@@ -197,46 +225,62 @@
 
     held = (g, depth_kernel, point_weight, gain[None], bias[None])
     near_g, near_k, near_w, gain, bias = call(
-        stage_kernel, [out(a.shape, a.dtype) for a in held], "stage", 4 * width * width * 8, *held
+        stage_kernel, [out(a.shape, a.dtype) for a in held], 4 * width * width * 8, *held
     )
     x = lax.all_to_all(acts[:, 0], SP, 0, 0, tiled=True)
     d, p, stats = call(
         forward_kernel,
         [pltpu.HBM((places, width), BF), out((places, width), F32), out((n, 4, width), F32)],
-        "forward", 2 * places * width * width, x, near_g, near_k, near_w,
+        2 * places * width * width, x, near_g, near_k, near_w,
     )
     stats = lax.all_to_all(stats, SP, 0, 0, tiled=True)
     (picked,) = call(
-        lambda *refs: pick_kernel(n, *refs), [out((2 * n * half, places), BF)], "pick",
+        lambda *refs: pick_kernel(n, *refs), [out((2 * n * half, places), BF)],
         4 * places * width * n * half, d, far=(0,),
     )
     coefs, dp, other = call(
         lambda *refs: project_kernel(float(count), *refs),
         [out((2, width), F32), out((places, width), BF), out((n, half, width), BF)],
-        "project", 2 * places * width * n * half, stats, p, g, gain, picked,
+        2 * places * width * n * half, stats, p, g, gain, picked,
     )
     other = lax.ppermute(other, "core", [(0, 1), (1, 0)])
-    own, dinput, _ = call(
+    (own,) = call(
+        own_kernel, [out((n * half, width), F32)], 2 * places * width * n * half, dp, picked
+    )
+    (packed,) = call(pack_kernel, [out((n, half, width), BF)], n * half * width, own, other)
+    packed = lax.all_to_all(packed, SP, 0, 0, tiled=True)
+    keep, send, _ = call(
         input_kernel,
-        [out((n * half, width), F32), out((rows, cols, width), BF), out((places, width), F32)],
-        "input", 4 * places * width * width, dp, picked, point_weight, depth_kernel, g, x, far=(2,),
-    )
-    (packed,) = call(
-        pack_kernel, [out((n, half + cols, width), BF)], "pack", n * half * width, own, other, dinput
-    )
-    packed = lax.all_to_all(packed, SP, 0, 0, tiled=True)
+        [
+            out((rows // 2, cols, width), BF),
+            out((rows // 2, cols, width), BF),
+            out((places, width), F32),
+        ],
+        4 * places * width * width, dp, point_weight, depth_kernel, g, x, far=(1,),
+    )
+    got = lax.ppermute(send, "yh", [(0, 1), (1, 0)])
+    ring = lax.axis_size("x")
+    turned = call(
+        turn_kernel, [jax.ShapeDtypeStruct((2, cols, width), BF)] * ring,
+        places * width, keep, got,
+    )
+    arrived = [turned[0]]
+    for k in range(1, ring):
+        pairs = [(i, (i + k) % ring) for i in range(ring)]
+        arrived.append(lax.ppermute(turned[k], "x", pairs))
+    (input_grad,) = call(
+        place_kernel, [jax.ShapeDtypeStruct((rows, cols, width), BF)],
+        places * width, *arrived,
+    )
+    input_grad = input_grad[:, None]
     (block_out,) = call(
-        output_kernel, [out((rows, cols, width), BF)], "output", 4 * places * width,
+        output_kernel, [out((rows, cols, width), BF)], 4 * places * width,
         x, p, coefs, gain, bias,
     )
     each = -(-half // lines)
-    (pieces,) = call(
-        slice_kernel, [out((lines, each, width), F32)], "slice", n * half * width, packed
-    )
+    (pieces,) = call(slice_kernel, [out((lines, each, width), F32)], n * half * width, packed)
     pieces = lax.all_to_all(pieces, LINE, 0, 0, tiled=True)
-    (summed,) = call(
-        copies_kernel, [out((copies, each, width), F32)], "copies", width * width, pieces
-    )
+    (summed,) = call(copies_kernel, [out((copies, each, width), F32)], width * width, pieces)
     whole = lax.all_to_all(summed, GRP, 0, 0, tiled=True)
     whole = whole.reshape(lines, 2, each, width).swapaxes(1, 2).reshape(-1)
     span = width * width // n
@@ -246,7 +290,6 @@
         weight_grad = jnp.where(odd, whole[width // 2 : width // 2 + span], whole[:span])
     else:
         weight_grad = lax.dynamic_slice(whole, (shift,), (span,))
-    input_grad = packed[:, half:, :][:, None]
     return block_out[None], input_grad, weight_grad
 
 
@@ -255,4 +298,5 @@
     fine = Mesh(mesh.devices.reshape(sizes), ("yl", "z", "core", "x", "yh"))
     in_specs = (P(GRP, SP, None, None), P(GRP + SP, None, None, None), P(), P(), P(), P())
     out_specs = (P(GRP + SP, None, None, None), P(GRP, SP, None, None), P(SP))
+
     return jax.shard_map(body, mesh=fine, in_specs=in_specs, out_specs=out_specs, check_vma=False)

time: 142 us -> 171 us (1.20)
  the two profiles are of different devices: /device:TPU:1 before, /device:TPU:46 now
where the time goes in v3:
time: 171 us; the launch traced here: 170 us
  blocking collectives  56.4 us (33%)
  starting transfers between devices  55.7 us (33%)
  waiting for transfers between devices  41 us (24%)
  Pallas kernels  9.51 us (6%)
  local copies, waits for them, and re-layouts  5.31 us (3%)
    all_to_all x1, blocking collectives, body(): pieces = lax.all_to_all(pieces, LINE, 0, 0, tiled=True)  28.4 us
    all_to_all x1, blocking collectives, body(): packed = lax.all_to_all(packed, SP, 0, 0, tiled=True)  28 us
    ppermute x7, starting transfers between devices, body(): arrived.append(lax.ppermute(turned[k], 'x', pairs))  27 us
    ppermute x1, waiting for transfers between devices, body(): got = lax.ppermute(send, 'yh', [(0, 1), (1, 0)])  14 us
    all_to_all x1, waiting for transfers between devices, body(): x = lax.all_to_all(acts[:, 0], SP, 0, 0, tiled=True)  11.1 us
    all_to_all x1, starting transfers between devices, body(): x = lax.all_to_all(acts[:, 0], SP, 0, 0, tiled=True)  11.1 us
    all_to_all x1, waiting for transfers between devices, body(): stats = lax.all_to_all(stats, SP, 0, 0, tiled=True)  9.97 us
    pallas_call x12, Pallas kernels, call(): pl.pallas_call(kernel, out_shape=outs, in_specs=[VMEM] * len(args), out_s...  9.51 us
  transfers between devices with their start and end apart: 12, of which 6 were waited for; matrix products, arithmetic and copies ran while one was open for 1% of the time, Pallas kernels for 4%

profile of v3, /device:TPU:46, one launch (start us, length us, event | category | flops | bytes accessed | tf_op | source)
XLA Modules:
  0.0 169.9 jit_solution(9892508245405550801)
XLA Ops:
  0.6 11.1 %all-to-all-start = ((bf16[16,16,728]{2,1,0:T(8,128)(2,1)}), bf16[16,16,728]{2,1,0:T(8,128)(2,1)S(1)}, u32[]{:S(2)}, u32[]{:S(2)}) async-start(bf16[16,16,728]{2,1,0:T(8,128)(2,1)} %bitcast.10), calls=%async_computation | async-start | bytes 786432 | tf_op jit(solution)/shard_map/all_to_all | solution.py:230
  11.7 0.7 broadcast_in_dim.12.refs_3_
  12.4 0.7 broadcast_in_dim.13.refs_4_
  13.1 1.2 copy-done
  14.3 1.0 copy-done.1
  15.3 0.8 copy-done.3
  16.2 11.1 %all-to-all-done.x_ref = bf16[16,16,728]{2,1,0:T(8,128)(2,1)S(1)} async-done(((bf16[16,16,728]{2,1,0:T(8,128)(2,1)}), bf16[16,16,728]{2,1,0:T(8,128)(2,1)S(1)}, u32[]{:S(2)}, u32[]{:S(2)}) %all-to-all-start) | async-done | bytes 372768 | tf_op jit(solution)/shard_map/all_to_all | solution.py:230
  27.3 1.8 %shard_map.86 = (bf16[256,728]{1,0:T(8,128)(2,1)}, f32[256,728]{1,0:T(8,128)S(1)}, f32[16,4,728]{2,1,0:T(4,128)}) custom-call(bf16[16,16,728]{2,1,0:T(8,128)(2,1)S(1)} %all-to-all-done.x_ref, bf16[16,16,728]{2,1,0:T(8,128)(2,1)S(1)} %get-tuple-element.24.g_ref, f32[3,3,728]{2,1,0:T(4,128)S(1)} %get-tuple-element.25.k_ref, ...), custom_call_target="tpu_custom_call" | custom-call | flops 271351808 | bytes 3136224 | tf_op jit(solution)/shard_map/pallas_call | solution.py:24
  29.1 6.7 %all-to-all-start.1 = ((f32[16,4,728]{2,1,0:T(4,128)}), f32[16,4,728]{2,1,0:T(4,128)S(1)}, u32[]{:S(2)}, u32[]{:S(2)}) async-start(f32[16,4,728]{2,1,0:T(4,128)} %get-tuple-element.28), calls=%async_computation.1 | async-start | bytes 393216 | tf_op jit(solution)/shard_map/all_to_all | solution.py:236
  35.8 1.5 shard_map.87.refs_4_.t_ref
  37.4 10.0 %all-to-all-done.1.refs_0_ = f32[16,4,728]{2,1,0:T(4,128)S(1)} async-done(((f32[16,4,728]{2,1,0:T(4,128)}), f32[16,4,728]{2,1,0:T(4,128)S(1)}, u32[]{:S(2)}, u32[]{:S(2)}) %all-to-all-start.1) | async-done | bytes 186400 | tf_op jit(solution)/shard_map/all_to_all | solution.py:236
  48.0 1.9 %collective-permute-start.8 = (bf16[16,24,728]{2,1,0:T(8,128)(2,1)S(1)}, bf16[16,24,728]{2,1,0:T(8,128)(2,1)S(1)}, u32[]{:S(2)}, u32[]{:S(2)}) collective-permute-start(bf16[16,24,728]{2,1,0:T(8,128)(2,1)S(1)} %get-tuple-element.44), channel_id=1, source_target_pairs={{0,16},{16,0},{1,17},{17,1},{2,18},{18,2},{3,19},{19,3},{4,20},{20... | collective-permute-start | bytes 1677320 | tf_op jit(solution)/shard_map/ppermute | solution.py:246
  50.2 1.7 collective-permute-done.8.r_ref
  52.0 28.0 %all_to_all.25.b_ref = bf16[16,24,728]{2,1,0:T(8,128)(2,1)S(1)} all-to-all(bf16[16,24,728]{2,1,0:T(8,128)(2,1)S(1)} %shard_map.94), channel_id=1, replica_groups=mesh['yl'=4,'z'=8,'core'=2,'x'=8,'yh'=2] {'x','yh'}, dimensions={0} | all-to-all | bytes 1118208 | tf_op jit(solution)/shard_map/all_to_all | solution.py:251
  80.1 28.4 %all_to_all.26.b_ref = f32[32,1,728]{2,1,0:T(1,128)S(1)} all-to-all(f32[32,1,728]{2,1,0:T(1,128)S(1)} %shard_map.95), channel_id=1, replica_groups=mesh['yl'=4,'z'=8,'core'=2,'x'=8,'yh'=2] {'yl','z'}, dimensions={0} | all-to-all | bytes 186368 | tf_op jit(solution)/shard_map/all_to_all | solution.py:282
  108.5 0.7 shard_map.96
  109.2 6.4 %all-to-all-start.4 = ((f32[64,1,728]{2,1,0:T(1,128)}), f32[64,1,728]{2,1,0:T(1,128)S(1)}, u32[]{:S(2)}, u32[]{:S(2)}) async-start(f32[64,1,728]{2,1,0:T(1,128)} %shard_map.96), calls=%async_computation.4 | async-start | bytes 393216 | tf_op jit(solution)/shard_map/all_to_all | solution.py:284
  115.6 3.2 %shard_map.90 = (bf16[8,16,728]{2,1,0:T(8,128)(2,1)S(1)}, bf16[8,16,728]{2,1,0:T(8,128)(2,1)S(1)}, f32[256,728]{1,0:T(8,128)}) custom-call(bf16[256,728]{1,0:T(8,128)(2,1)S(1)} %get-tuple-element.33.dp_ref, bf16[728,728]{1,0:T(8,128)(2,1)} %w_ref.1, f32[3,3,728]{2,1,0:T(4,128)S(1)} %copy-done.4, bf16[16,16,728]{2,1,0:T(8,128)(2,1)S(1)} %bitcast.9, ...), custom_call_target="tpu_custom_call" | custom-call | flops 542703616 | bytes 3322592 | tf_op jit(solution)/shard_map/pallas_call | solution.py:24
  118.8 2.5 %collective-permute-start = (bf16[8,16,728]{2,1,0:T(8,128)(2,1)S(1)}, bf16[8,16,728]{2,1,0:T(8,128)(2,1)S(1)}, u32[]{:S(2)}, u32[]{:S(2)}) collective-permute-start(bf16[8,16,728]{2,1,0:T(8,128)(2,1)S(1)} %get-tuple-element.35), channel_id=1, source_target_pairs={{0,1},{1,0},{2,3},{3,2},{4,5},{5,4},{6,7},{7,6},{8,9},{9,8},{10,11... | collective-permute-start | bytes 559112 | tf_op jit(solution)/shard_map/ppermute | solution.py:261
  121.3 14.0 %collective-permute-done.got_ref = bf16[8,16,728]{2,1,0:T(8,128)(2,1)S(1)} collective-permute-done((bf16[8,16,728]{2,1,0:T(8,128)(2,1)S(1)}, bf16[8,16,728]{2,1,0:T(8,128)(2,1)S(1)}, u32[]{:S(2)}, u32[]{:S(2)}) %collective-permute-start) | collective-permute-done | bytes 186400 | tf_op jit(solution)/shard_map/ppermute | solution.py:261
  135.4 4.3 %collective-permute-start.1 = (bf16[2,16,728]{2,1,0:T(8,128)(2,1)S(1)}, bf16[2,16,728]{2,1,0:T(8,128)(2,1)S(1)}, u32[]{:S(2)}, u32[]{:S(2)}) collective-permute-start(bf16[2,16,728]{2,1,0:T(8,128)(2,1)S(1)} %get-tuple-element.37), channel_id=1, source_target_pairs={{0,2},{2,4},{4,6},{6,8},{8,10},{10,12},{12,14},{14,0},{1,3},{3,5},... | collective-permute-start | bytes 139784 | tf_op jit(solution)/shard_map/ppermute | solution.py:270
  139.7 2.9 %collective-permute-start.2 = (bf16[2,16,728]{2,1,0:T(8,128)(2,1)S(1)}, bf16[2,16,728]{2,1,0:T(8,128)(2,1)S(1)}, u32[]{:S(2)}, u32[]{:S(2)}) collective-permute-start(bf16[2,16,728]{2,1,0:T(8,128)(2,1)S(1)} %get-tuple-element.38), channel_id=1, source_target_pairs={{0,4},{2,6},{4,8},{6,10},{8,12},{10,14},{12,0},{14,2},{1,5},{3,7},... | collective-permute-start | bytes 139784 | tf_op jit(solution)/shard_map/ppermute | solution.py:270
  142.6 4.5 %collective-permute-start.3 = (bf16[2,16,728]{2,1,0:T(8,128)(2,1)S(1)}, bf16[2,16,728]{2,1,0:T(8,128)(2,1)S(1)}, u32[]{:S(2)}, u32[]{:S(2)}) collective-permute-start(bf16[2,16,728]{2,1,0:T(8,128)(2,1)S(1)} %get-tuple-element.39), channel_id=1, source_target_pairs={{0,6},{2,8},{4,10},{6,12},{8,14},{10,0},{12,2},{14,4},{1,7},{3,9},... | collective-permute-start | bytes 139784 | tf_op jit(solution)/shard_map/ppermute | solution.py:270
  147.1 5.3 %collective-permute-start.4 = (bf16[2,16,728]{2,1,0:T(8,128)(2,1)S(1)}, bf16[2,16,728]{2,1,0:T(8,128)(2,1)S(1)}, u32[]{:S(2)}, u32[]{:S(2)}) collective-permute-start(bf16[2,16,728]{2,1,0:T(8,128)(2,1)S(1)} %get-tuple-element.40), channel_id=1, source_target_pairs={{0,8},{2,10},{4,12},{6,14},{8,0},{10,2},{12,4},{14,6},{1,9},{3,11}... | collective-permute-start | bytes 139784 | tf_op jit(solution)/shard_map/ppermute | solution.py:270
  152.5 3.1 %collective-permute-start.5 = (bf16[2,16,728]{2,1,0:T(8,128)(2,1)S(1)}, bf16[2,16,728]{2,1,0:T(8,128)(2,1)S(1)}, u32[]{:S(2)}, u32[]{:S(2)}) collective-permute-start(bf16[2,16,728]{2,1,0:T(8,128)(2,1)S(1)} %get-tuple-element.41), channel_id=1, source_target_pairs={{0,10},{2,12},{4,14},{6,0},{8,2},{10,4},{12,6},{14,8},{1,11},{3,13... | collective-permute-start | bytes 139784 | tf_op jit(solution)/shard_map/ppermute | solution.py:270
  155.6 5.0 %collective-permute-start.6 = (bf16[2,16,728]{2,1,0:T(8,128)(2,1)S(1)}, bf16[2,16,728]{2,1,0:T(8,128)(2,1)S(1)}, u32[]{:S(2)}, u32[]{:S(2)}) collective-permute-start(bf16[2,16,728]{2,1,0:T(8,128)(2,1)S(1)} %get-tuple-element.42), channel_id=1, source_target_pairs={{0,12},{2,14},{4,0},{6,2},{8,4},{10,6},{12,8},{14,10},{1,13},{3,15... | collective-permute-start | bytes 139784 | tf_op jit(solution)/shard_map/ppermute | solution.py:270
  160.5 1.9 %collective-permute-start.7 = (bf16[2,16,728]{2,1,0:T(8,128)(2,1)S(1)}, bf16[2,16,728]{2,1,0:T(8,128)(2,1)S(1)}, u32[]{:S(2)}, u32[]{:S(2)}) collective-permute-start(bf16[2,16,728]{2,1,0:T(8,128)(2,1)S(1)} %get-tuple-element.43), channel_id=1, source_target_pairs={{0,14},{2,0},{4,2},{6,4},{8,6},{10,8},{12,10},{14,12},{1,15},{3,1}... | collective-permute-start | bytes 139784 | tf_op jit(solution)/shard_map/ppermute | solution.py:270
  162.7 0.7 copy.10
  163.5 0.7 collective-permute-done.6.refs_6_
  164.2 3.6 %collective-permute-done.7.refs_7_ = bf16[2,16,728]{2,1,0:T(8,128)(2,1)S(1)} collective-permute-done((bf16[2,16,728]{2,1,0:T(8,128)(2,1)S(1)}, bf16[2,16,728]{2,1,0:T(8,128)(2,1)S(1)}, u32[]{:S(2)}, u32[]{:S(2)}) %collective-permute-start.7) | collective-permute-done | bytes 46624 | tf_op jit(solution)/shard_map/ppermute | solution.py:270
  167.7 0.8 shard_map.92
  169.2 0.8 slice_select_fusion
  (22 shorter events, 2.1 us)
Async XLA Ops:
  0.6 26.7 %all-to-all-start = ((bf16[16,16,728]{2,1,0:T(8,128)(2,1)}), bf16[16,16,728]{2,1,0:T(8,128)(2,1)S(1)}, u32[]{:S(2)}, u32[]{:S(2)}) async-start(bf16[16,16,728]{2,1,0:T(8,128)(2,1)} %bitcast.10), calls=%async_computation | async-start | bytes 786432 | tf_op jit(solution)/shard_map/all_to_all | solution.py:230
  13.1 1.2 copy-start
  14.3 1.0 copy-start.1
  15.3 0.8 copy-start.3
  29.1 18.2 %copy-start.2 = (bf16[1,16,16,728]{3,2,1,0:T(8,128)(2,1)S(1)}, bf16[1,16,16,728]{3,2,1,0:T(8,128)(2,1)}, u32[]{:S(2)}) copy-start(bf16[1,16,16,728]{3,2,1,0:T(8,128)(2,1)} %param.7) | copy-start | bytes 1118212
  29.1 18.2 %all-to-all-start.1 = ((f32[16,4,728]{2,1,0:T(4,128)}), f32[16,4,728]{2,1,0:T(4,128)S(1)}, u32[]{:S(2)}, u32[]{:S(2)}) async-start(f32[16,4,728]{2,1,0:T(4,128)} %get-tuple-element.28), calls=%async_computation.1 | async-start | bytes 393216 | tf_op jit(solution)/shard_map/all_to_all | solution.py:236
  48.0 3.9 %collective-permute-start.8 = (bf16[16,24,728]{2,1,0:T(8,128)(2,1)S(1)}, bf16[16,24,728]{2,1,0:T(8,128)(2,1)S(1)}, u32[]{:S(2)}, u32[]{:S(2)}) collective-permute-start(bf16[16,24,728]{2,1,0:T(8,128)(2,1)S(1)} %get-tuple-element.44), channel_id=1, source_target_pairs={{0,16},{16,0},{1,17},{17,1},{2,18},{18,2},{3,19},{19,3},{4,20},{20... | collective-permute-start | bytes 1677320 | tf_op jit(solution)/shard_map/ppermute | solution.py:246
  52.0 63.7 %copy-start.4 = (f32[3,3,728]{2,1,0:T(4,128)S(1)}, f32[3,3,728]{2,1,0:T(4,128)}, u32[]{:S(2)}) copy-start(f32[3,3,728]{2,1,0:T(4,128)} %k_ref.1) | copy-start | bytes 78628
  109.2 59.3 %all-to-all-start.4 = ((f32[64,1,728]{2,1,0:T(1,128)}), f32[64,1,728]{2,1,0:T(1,128)S(1)}, u32[]{:S(2)}, u32[]{:S(2)}) async-start(f32[64,1,728]{2,1,0:T(1,128)} %shard_map.96), calls=%async_computation.4 | async-start | bytes 393216 | tf_op jit(solution)/shard_map/all_to_all | solution.py:284
  118.8 16.5 %collective-permute-start = (bf16[8,16,728]{2,1,0:T(8,128)(2,1)S(1)}, bf16[8,16,728]{2,1,0:T(8,128)(2,1)S(1)}, u32[]{:S(2)}, u32[]{:S(2)}) collective-permute-start(bf16[8,16,728]{2,1,0:T(8,128)(2,1)S(1)} %get-tuple-element.35), channel_id=1, source_target_pairs={{0,1},{1,0},{2,3},{3,2},{4,5},{5,4},{6,7},{7,6},{8,9},{9,8},{10,11... | collective-permute-start | bytes 559112 | tf_op jit(solution)/shard_map/ppermute | solution.py:261
  135.4 20.1 %collective-permute-start.1 = (bf16[2,16,728]{2,1,0:T(8,128)(2,1)S(1)}, bf16[2,16,728]{2,1,0:T(8,128)(2,1)S(1)}, u32[]{:S(2)}, u32[]{:S(2)}) collective-permute-start(bf16[2,16,728]{2,1,0:T(8,128)(2,1)S(1)} %get-tuple-element.37), channel_id=1, source_target_pairs={{0,2},{2,4},{4,6},{6,8},{8,10},{10,12},{12,14},{14,0},{1,3},{3,5},... | collective-permute-start | bytes 139784 | tf_op jit(solution)/shard_map/ppermute | solution.py:270
  139.7 20.8 %collective-permute-start.2 = (bf16[2,16,728]{2,1,0:T(8,128)(2,1)S(1)}, bf16[2,16,728]{2,1,0:T(8,128)(2,1)S(1)}, u32[]{:S(2)}, u32[]{:S(2)}) collective-permute-start(bf16[2,16,728]{2,1,0:T(8,128)(2,1)S(1)} %get-tuple-element.38), channel_id=1, source_target_pairs={{0,4},{2,6},{4,8},{6,10},{8,12},{10,14},{12,0},{14,2},{1,5},{3,7},... | collective-permute-start | bytes 139784 | tf_op jit(solution)/shard_map/ppermute | solution.py:270
  142.6 20.8 %collective-permute-start.3 = (bf16[2,16,728]{2,1,0:T(8,128)(2,1)S(1)}, bf16[2,16,728]{2,1,0:T(8,128)(2,1)S(1)}, u32[]{:S(2)}, u32[]{:S(2)}) collective-permute-start(bf16[2,16,728]{2,1,0:T(8,128)(2,1)S(1)} %get-tuple-element.39), channel_id=1, source_target_pairs={{0,6},{2,8},{4,10},{6,12},{8,14},{10,0},{12,2},{14,4},{1,7},{3,9},... | collective-permute-start | bytes 139784 | tf_op jit(solution)/shard_map/ppermute | solution.py:270
  147.1 16.3 %collective-permute-start.4 = (bf16[2,16,728]{2,1,0:T(8,128)(2,1)S(1)}, bf16[2,16,728]{2,1,0:T(8,128)(2,1)S(1)}, u32[]{:S(2)}, u32[]{:S(2)}) collective-permute-start(bf16[2,16,728]{2,1,0:T(8,128)(2,1)S(1)} %get-tuple-element.40), channel_id=1, source_target_pairs={{0,8},{2,10},{4,12},{6,14},{8,0},{10,2},{12,4},{14,6},{1,9},{3,11}... | collective-permute-start | bytes 139784 | tf_op jit(solution)/shard_map/ppermute | solution.py:270
  152.5 11.0 %collective-permute-start.5 = (bf16[2,16,728]{2,1,0:T(8,128)(2,1)S(1)}, bf16[2,16,728]{2,1,0:T(8,128)(2,1)S(1)}, u32[]{:S(2)}, u32[]{:S(2)}) collective-permute-start(bf16[2,16,728]{2,1,0:T(8,128)(2,1)S(1)} %get-tuple-element.41), channel_id=1, source_target_pairs={{0,10},{2,12},{4,14},{6,0},{8,2},{10,4},{12,6},{14,8},{1,11},{3,13... | collective-permute-start | bytes 139784 | tf_op jit(solution)/shard_map/ppermute | solution.py:270
  155.6 8.6 %collective-permute-start.6 = (bf16[2,16,728]{2,1,0:T(8,128)(2,1)S(1)}, bf16[2,16,728]{2,1,0:T(8,128)(2,1)S(1)}, u32[]{:S(2)}, u32[]{:S(2)}) collective-permute-start(bf16[2,16,728]{2,1,0:T(8,128)(2,1)S(1)} %get-tuple-element.42), channel_id=1, source_target_pairs={{0,12},{2,14},{4,0},{6,2},{8,4},{10,6},{12,8},{14,10},{1,13},{3,15... | collective-permute-start | bytes 139784 | tf_op jit(solution)/shard_map/ppermute | solution.py:270
  160.5 7.2 %collective-permute-start.7 = (bf16[2,16,728]{2,1,0:T(8,128)(2,1)S(1)}, bf16[2,16,728]{2,1,0:T(8,128)(2,1)S(1)}, u32[]{:S(2)}, u32[]{:S(2)}) collective-permute-start(bf16[2,16,728]{2,1,0:T(8,128)(2,1)S(1)} %get-tuple-element.43), channel_id=1, source_target_pairs={{0,14},{2,0},{4,2},{6,4},{8,6},{10,8},{12,10},{14,12},{1,15},{3,1}... | collective-permute-start | bytes 139784 | tf_op jit(solution)/shard_map/ppermute | solution.py:270

commit v4 on v2

--- a/solution.py
+++ b/solution.py
@@ -181,6 +181,26 @@
         o_ref[k] = total
 
 
+def final_kernel(b_ref, o_ref):
+    span = o_ref.shape[0]
+    width = b_ref.shape[-1]
+    odd = lax.rem(lax.axis_index("yh"), 2) == 1
+    half = width // 2
+    each = b_ref.shape[1]
+
+    def row_at(r):
+        q = r // 2 % each
+        return b_ref[r // 2 // each * 2 + r % 2, q : q + 1, :]
+
+    for r in range(-(-span // width)):
+        row = row_at(r)
+        after = row_at(r + 1)
+        late = jnp.concatenate([row[:, half:], after[:, :half]], axis=1)
+        line = jnp.where(odd, late, row).reshape(width)
+        size = min(width, span - r * width)
+        o_ref[r * width : r * width + size] = line[:size]
+
+
 def out(shape, dtype):
     return pltpu.VMEM(shape, dtype)
 
@@ -219,7 +239,7 @@
     own, dinput, _ = call(
         input_kernel,
         [out((n * half, width), F32), out((rows, cols, width), BF), out((places, width), F32)],
-        "input", 4 * places * width * width, dp, picked, point_weight, depth_kernel, g, x, far=(2,),
+        "input", 4 * places * width * width, dp, picked, point_weight, depth_kernel, g, x,
     )
     (packed,) = call(
         pack_kernel, [out((n, half + cols, width), BF)], "pack", n * half * width, own, other, dinput
@@ -238,14 +258,10 @@
         copies_kernel, [out((copies, each, width), F32)], "copies", width * width, pieces
     )
     whole = lax.all_to_all(summed, GRP, 0, 0, tiled=True)
-    whole = whole.reshape(lines, 2, each, width).swapaxes(1, 2).reshape(-1)
-    span = width * width // n
-    shift = (lax.axis_index(SP) * span) % width
-    if (2 * span) % width == 0:
-        odd = shift != 0
-        weight_grad = jnp.where(odd, whole[width // 2 : width // 2 + span], whole[:span])
-    else:
-        weight_grad = lax.dynamic_slice(whole, (shift,), (span,))
+    (weight_grad,) = call(
+        final_kernel, [jax.ShapeDtypeStruct((width * width // n,), F32)], "final", width * width,
+        whole,
+    )
     input_grad = packed[:, half:, :][:, None]
     return block_out[None], input_grad, weight_grad
 

time: 142 us -> 142 us (level)
  Pallas kernels: 8.5 us -> 10.3 us
    pallas_call x9 -> x10, Pallas kernels: 8.5 us -> 10.3 us  [call(): pl.pallas_call(kernel, out_shape=outs, in_specs=[VMEM] * len(args), out_s...]
    unnamed x12 -> x14, local copies, waits for them, and re-layouts: 4.54 us -> 4.55 us
  transfers between devices with their start and end apart: 4 -> 4, of which waited for: 3 -> 3; matrix products, arithmetic and copies ran while one was open for 2% -> 2% of each run, Pallas kernels for 4% -> 3%
where the time goes in v4:
time: 142 us; the launch traced here: 141 us
  blocking collectives  60.2 us (42%)
  starting transfers between devices  32.9 us (23%)
  waiting for transfers between devices  31.2 us (22%)
  Pallas kernels  10.3 us (7%)
  local copies, waits for them, and re-layouts  5.93 us (4%)
    all_to_all x1, blocking collectives, body(): packed = lax.all_to_all(packed, SP, 0, 0, tiled=True)  33 us
    all_to_all x1, blocking collectives, body(): pieces = lax.all_to_all(pieces, LINE, 0, 0, tiled=True)  27.2 us
    all_to_all x1, starting transfers between devices, body(): x = lax.all_to_all(acts[:, 0], SP, 0, 0, tiled=True)  13.1 us
    all_to_all x1, waiting for transfers between devices, body(): stats = lax.all_to_all(stats, SP, 0, 0, tiled=True)  11.6 us
    all_to_all x1, waiting for transfers between devices, body(): x = lax.all_to_all(acts[:, 0], SP, 0, 0, tiled=True)  10.7 us
    pallas_call x10, Pallas kernels, call(): pl.pallas_call(kernel, out_shape=outs, in_specs=[VMEM] * len(args), out_s...  10.3 us
    all_to_all x1, waiting for transfers between devices, body(): whole = lax.all_to_all(summed, GRP, 0, 0, tiled=True)  8.94 us
    ppermute x1, starting transfers between devices, body(): other = lax.ppermute(other, 'core', [(0, 1), (1, 0)])  8.71 us
  transfers between devices with their start and end apart: 4, of which 3 were waited for; matrix products, arithmetic and copies ran while one was open for 2% of the time, Pallas kernels for 3%

profile of v4, /device:TPU:1, one launch (start us, length us, event | category | flops | bytes accessed | tf_op | source)
XLA Modules:
  0.0 141.2 jit_solution(15091298859626478501)
XLA Ops:
  0.6 13.1 %all-to-all-start = ((bf16[16,16,728]{2,1,0:T(8,128)(2,1)}), bf16[16,16,728]{2,1,0:T(8,128)(2,1)S(1)}, u32[]{:S(2)}, u32[]{:S(2)}) async-start(bf16[16,16,728]{2,1,0:T(8,128)(2,1)} %bitcast.11), calls=%async_computation | async-start | bytes 786432 | tf_op jit(solution)/shard_map/all_to_all | solution.py:222
  13.8 0.7 broadcast_in_dim.12.refs_3_
  14.5 0.7 broadcast_in_dim.13.refs_4_
  15.2 1.2 copy-done
  16.4 1.0 copy-done.2
  17.4 0.8 copy-done.4
  18.2 0.1 stage.1
  18.3 10.7 %all-to-all-done.x_ref = bf16[16,16,728]{2,1,0:T(8,128)(2,1)S(1)} async-done(((bf16[16,16,728]{2,1,0:T(8,128)(2,1)}), bf16[16,16,728]{2,1,0:T(8,128)(2,1)S(1)}, u32[]{:S(2)}, u32[]{:S(2)}) %all-to-all-start) | async-done | bytes 372768 | tf_op jit(solution)/shard_map/all_to_all | solution.py:222
  28.9 1.8 %forward.1 = (bf16[256,728]{1,0:T(8,128)(2,1)}, f32[256,728]{1,0:T(8,128)S(1)}, f32[16,4,728]{2,1,0:T(4,128)}) custom-call(bf16[16,16,728]{2,1,0:T(8,128)(2,1)S(1)} %all-to-all-done.x_ref, bf16[16,16,728]{2,1,0:T(8,128)(2,1)S(1)} %get-tuple-element.16.g_ref, f32[3,3,728]{2,1,0:T(4,128)S(1)} %get-tuple-element.17.k_ref, ...), custom_call_target="tpu_custom_call" | custom-call | flops 271351808 | bytes 3136224 | tf_op jit(solution)/shard_map/forward/pallas_call | solution.py:24
  30.8 3.7 %all-to-all-start.1 = ((f32[16,4,728]{2,1,0:T(4,128)}), f32[16,4,728]{2,1,0:T(4,128)S(1)}, u32[]{:S(2)}, u32[]{:S(2)}) async-start(f32[16,4,728]{2,1,0:T(4,128)} %get-tuple-element.20), calls=%async_computation.1 | async-start | bytes 393216 | tf_op jit(solution)/shard_map/all_to_all | solution.py:228
  34.4 1.5 %pick.1.refs_4_.t_ref = bf16[768,256]{1,0:T(8,128)(2,1)S(1)} custom-call(bf16[256,728]{1,0:T(8,128)(2,1)} %get-tuple-element.22.refs_0_), custom_call_target="tpu_custom_call" | custom-call | flops 286261248 | bytes 765952 | tf_op jit(solution)/shard_map/pick/pallas_call | solution.py:24
  36.0 0.0 copy-start.1
  36.0 0.0 copy-start.5
  36.0 11.6 %all-to-all-done.1.refs_0_ = f32[16,4,728]{2,1,0:T(4,128)S(1)} async-done(((f32[16,4,728]{2,1,0:T(4,128)}), f32[16,4,728]{2,1,0:T(4,128)S(1)}, u32[]{:S(2)}, u32[]{:S(2)}) %all-to-all-start.1) | async-done | bytes 186400 | tf_op jit(solution)/shard_map/all_to_all | solution.py:228
  47.6 0.0 copy-done.3
  47.6 0.6 project.1
  48.2 8.7 %collective-permute-start = (bf16[16,24,728]{2,1,0:T(8,128)(2,1)S(1)}, bf16[16,24,728]{2,1,0:T(8,128)(2,1)S(1)}, u32[]{:S(2)}, u32[]{:S(2)}) collective-permute-start(bf16[16,24,728]{2,1,0:T(8,128)(2,1)S(1)} %get-tuple-element.27), channel_id=1, source_target_pairs={{0,16},{16,0},{1,17},{17,1},{2,18},{18,2},{3,19},{19,3},{4,20},{20... | collective-permute-start | bytes 1677320 | tf_op jit(solution)/shard_map/ppermute | solution.py:238
  56.9 0.0 copy-done.1
  56.9 0.0 copy-done.5
  56.9 2.0 %input.1 = (f32[384,728]{1,0:T(8,128)S(1)}, bf16[16,16,728]{2,1,0:T(8,128)(2,1)S(1)}, f32[256,728]{1,0:T(8,128)}) custom-call(bf16[256,728]{1,0:T(8,128)(2,1)S(1)} %get-tuple-element.25.dp_ref, bf16[768,256]{1,0:T(8,128)(2,1)S(1)} %pick.1.refs_4_.t_ref, bf16[728,728]{1,0:T(8,128)(2,1)S(1)} %copy-done.1, f32[3,3,728]{2,1,0:T(4,128)S(1)} %copy-done.5, ...), custom_call_target="tpu_custom_call" | custom-call | flops 542703616 | bytes 4834016 | tf_op jit(solution)/shard_map/input/pallas_call | solution.py:24
  59.0 0.0 collective-permute-done.r_ref
  59.0 0.1 pack.1
  59.1 33.0 %all_to_all.25.b_ref = bf16[16,40,728]{2,1,0:T(8,128)(2,1)S(1)} all-to-all(bf16[16,40,728]{2,1,0:T(8,128)(2,1)S(1)} %pack.1), channel_id=1, replica_groups=mesh['yl'=4,'z'=8,'core'=2,'x'=8,'yh'=2] {'x','yh'}, dimensions={0} | all-to-all | bytes 1863680 | tf_op jit(solution)/shard_map/all_to_all | solution.py:247
  92.0 0.1 slice.7
  92.1 27.2 %all_to_all.26.b_ref = f32[32,1,728]{2,1,0:T(1,128)S(1)} all-to-all(f32[32,1,728]{2,1,0:T(1,128)S(1)} %slice.7), channel_id=1, replica_groups=mesh['yl'=4,'z'=8,'core'=2,'x'=8,'yh'=2] {'yl','z'}, dimensions={0} | all-to-all | bytes 186368 | tf_op jit(solution)/shard_map/all_to_all | solution.py:256
  119.4 0.7 copies.1
  120.1 7.4 %all-to-all-start.4 = ((f32[64,1,728]{2,1,0:T(1,128)}), f32[64,1,728]{2,1,0:T(1,128)S(1)}, u32[]{:S(2)}, u32[]{:S(2)}) async-start(f32[64,1,728]{2,1,0:T(1,128)} %copies.1), calls=%async_computation.4 | async-start | bytes 393216 | tf_op jit(solution)/shard_map/all_to_all | solution.py:260
  127.5 0.2 output.1
  127.7 0.7 copy.10
  128.4 0.8 slice_bitcast_fusion
  129.2 8.9 %all-to-all-done.4.b_ref = f32[64,1,728]{2,1,0:T(1,128)S(1)} async-done(((f32[64,1,728]{2,1,0:T(1,128)}), f32[64,1,728]{2,1,0:T(1,128)S(1)}, u32[]{:S(2)}, u32[]{:S(2)}) %all-to-all-start.4) | async-done | bytes 186400 | tf_op jit(solution)/shard_map/all_to_all | solution.py:260
  138.1 3.0 %final.1 = f32[33124]{0:T(1024)} custom-call(f32[64,1,728]{2,1,0:T(1,128)S(1)} %all-to-all-done.4.b_ref), custom_call_target="tpu_custom_call" | custom-call | flops 529984 | bytes 318864 | tf_op jit(solution)/shard_map/final/pallas_call | solution.py:24
  (4 shorter events, 0.0 us)
Async XLA Ops:
  0.6 28.3 %all-to-all-start = ((bf16[16,16,728]{2,1,0:T(8,128)(2,1)}), bf16[16,16,728]{2,1,0:T(8,128)(2,1)S(1)}, u32[]{:S(2)}, u32[]{:S(2)}) async-start(bf16[16,16,728]{2,1,0:T(8,128)(2,1)} %bitcast.11), calls=%async_computation | async-start | bytes 786432 | tf_op jit(solution)/shard_map/all_to_all | solution.py:222
  15.1 1.2 copy-start
  16.4 1.0 copy-start.2
  17.4 0.8 copy-start.4
  30.8 16.8 %copy-start.3 = (bf16[1,16,16,728]{3,2,1,0:T(8,128)(2,1)S(1)}, bf16[1,16,16,728]{3,2,1,0:T(8,128)(2,1)}, u32[]{:S(2)}) copy-start(bf16[1,16,16,728]{3,2,1,0:T(8,128)(2,1)} %param.7) | copy-start | bytes 1118212
  30.8 16.8 %all-to-all-start.1 = ((f32[16,4,728]{2,1,0:T(4,128)}), f32[16,4,728]{2,1,0:T(4,128)S(1)}, u32[]{:S(2)}, u32[]{:S(2)}) async-start(f32[16,4,728]{2,1,0:T(4,128)} %get-tuple-element.20), calls=%async_computation.1 | async-start | bytes 393216 | tf_op jit(solution)/shard_map/all_to_all | solution.py:228
  36.0 20.9 %copy-start.1 = (bf16[728,728]{1,0:T(8,128)(2,1)S(1)}, bf16[728,728]{1,0:T(8,128)(2,1)}, u32[]{:S(2)}) copy-start(bf16[728,728]{1,0:T(8,128)(2,1)} %w_ref.1) | copy-start | bytes 3179908
  36.0 20.9 %copy-start.5 = (f32[3,3,728]{2,1,0:T(4,128)S(1)}, f32[3,3,728]{2,1,0:T(4,128)}, u32[]{:S(2)}) copy-start(f32[3,3,728]{2,1,0:T(4,128)} %k_ref.1) | copy-start | bytes 78628
  48.2 10.8 %collective-permute-start = (bf16[16,24,728]{2,1,0:T(8,128)(2,1)S(1)}, bf16[16,24,728]{2,1,0:T(8,128)(2,1)S(1)}, u32[]{:S(2)}, u32[]{:S(2)}) collective-permute-start(bf16[16,24,728]{2,1,0:T(8,128)(2,1)S(1)} %get-tuple-element.27), channel_id=1, source_target_pairs={{0,16},{16,0},{1,17},{17,1},{2,18},{18,2},{3,19},{19,3},{4,20},{20... | collective-permute-start | bytes 1677320 | tf_op jit(solution)/shard_map/ppermute | solution.py:238
  120.1 18.0 %all-to-all-start.4 = ((f32[64,1,728]{2,1,0:T(1,128)}), f32[64,1,728]{2,1,0:T(1,128)S(1)}, u32[]{:S(2)}, u32[]{:S(2)}) async-start(f32[64,1,728]{2,1,0:T(1,128)} %copies.1), calls=%async_computation.4 | async-start | bytes 393216 | tf_op jit(solution)/shard_map/all_to_all | solution.py:260

commit v5 on v2

--- a/solution.py
+++ b/solution.py
@@ -11,6 +11,7 @@
 SP = ("x", "yh")
 LINE = ("yl", "z")
 GRP = ("yl", "z", "core")
+PAIR = ("z", "core")
 VMEM = pl.BlockSpec(memory_space=pltpu.VMEM)
 
 
@@ -82,7 +83,7 @@
             s_ref[k, :, a:b] = stats
 
 
-def pick_kernel(parts, d_ref, t_ref):
+def pick_kernel(parts, each, d_ref, t_ref):
     width = d_ref.shape[1]
     lines = t_ref.shape[0]
     part = lines // 2 // parts
@@ -92,7 +93,9 @@
     other = line >= lines // 2
     line = jnp.where(other, line - lines // 2, line)
     slot = (line * (65536 // part + 1)) >> 16
-    row = 2 * (line - part * slot) + jnp.where(other, 1 - core, core)
+    inner = line - part * slot
+    block = (inner * (65536 // each + 1)) >> 16
+    row = inner + each * (block + jnp.where(other, 1 - core, core))
     source = ((slot * (2 * width // parts)) >> 1) + row
     source = jnp.where(row < per, source, -1)
     chan = lax.broadcasted_iota(jnp.int32, (lines, width), 1)
@@ -165,18 +168,14 @@
     for k in range(1, n):
         total = total + b_ref[k, :part, :].astype(F32)
     for k in range(lines):
-        for q in range(per):
-            r = k * per + q
-            if r < part:
-                o_ref[k, q : q + 1, :] = total[r : r + 1, :]
-            else:
-                o_ref[k, q : q + 1, :] = jnp.zeros((1, width), F32)
+        at = k % (part // per) * per
+        o_ref[k] = total[at : at + per, :].astype(BF)
 
 
 def copies_kernel(b_ref, o_ref):
-    total = b_ref[0]
+    total = b_ref[0].astype(F32)
     for k in range(1, b_ref.shape[0]):
-        total = total + b_ref[k]
+        total = total + b_ref[k].astype(F32)
     for k in range(o_ref.shape[0]):
         o_ref[k] = total
 
@@ -188,11 +187,12 @@
 def body(acts, cotangent, depth_kernel, point_weight, gain, bias):
     n = lax.axis_size(SP)
     lines = lax.axis_size(LINE)
-    copies = lax.axis_size(GRP)
     _, rows, cols, width = cotangent.shape
     places = rows * cols
     count = places * n
     half = -(-(-(-width // n) // 2) // 8) * 8
+    blocks = lax.axis_size("z")
+    each = half // blocks
     g = cotangent[0]
 
     held = (g, depth_kernel, point_weight, gain[None], bias[None])
@@ -207,7 +207,7 @@
     )
     stats = lax.all_to_all(stats, SP, 0, 0, tiled=True)
     (picked,) = call(
-        lambda *refs: pick_kernel(n, *refs), [out((2 * n * half, places), BF)], "pick",
+        lambda *refs: pick_kernel(n, each, *refs), [out((2 * n * half, places), BF)], "pick",
         4 * places * width * n * half, d, far=(0,),
     )
     coefs, dp, other = call(
@@ -219,7 +219,7 @@
     own, dinput, _ = call(
         input_kernel,
         [out((n * half, width), F32), out((rows, cols, width), BF), out((places, width), F32)],
-        "input", 4 * places * width * width, dp, picked, point_weight, depth_kernel, g, x, far=(2,),
+        "input", 4 * places * width * width, dp, picked, point_weight, depth_kernel, g, x,
     )
     (packed,) = call(
         pack_kernel, [out((n, half + cols, width), BF)], "pack", n * half * width, own, other, dinput
@@ -229,16 +229,15 @@
         output_kernel, [out((rows, cols, width), BF)], "output", 4 * places * width,
         x, p, coefs, gain, bias,
     )
-    each = -(-half // lines)
     (pieces,) = call(
-        slice_kernel, [out((lines, each, width), F32)], "slice", n * half * width, packed
+        slice_kernel, [out((lines, each, width), BF)], "slice", n * half * width, packed
     )
     pieces = lax.all_to_all(pieces, LINE, 0, 0, tiled=True)
     (summed,) = call(
-        copies_kernel, [out((copies, each, width), F32)], "copies", width * width, pieces
-    )
-    whole = lax.all_to_all(summed, GRP, 0, 0, tiled=True)
-    whole = whole.reshape(lines, 2, each, width).swapaxes(1, 2).reshape(-1)
+        copies_kernel, [out((2 * blocks, each, width), F32)], "copies", width * width, pieces
+    )
+    whole = lax.all_to_all(summed, PAIR, 0, 0, tiled=True)
+    whole = whole.reshape(-1)
     span = width * width // n
     shift = (lax.axis_index(SP) * span) % width
     if (2 * span) % width == 0:

time: 142 us -> 139 us (0.979)
    unnamed x12 -> x14, local copies, waits for them, and re-layouts: 4.54 us -> 4.55 us
  transfers between devices with their start and end apart: 4 -> 4, of which waited for: 3 -> 3; matrix products, arithmetic and copies ran while one was open for 2% -> 2% of each run, Pallas kernels for 4% -> 3%
where the time goes in v5:
time: 139 us; the launch traced here: 138 us
  blocking collectives  60.7 us (44%)
  starting transfers between devices  32 us (23%)
  waiting for transfers between devices  30.7 us (22%)
  Pallas kernels  7.31 us (5%)
  local copies, waits for them, and re-layouts  6.1 us (4%)
    all_to_all x1, blocking collectives, body(): packed = lax.all_to_all(packed, SP, 0, 0, tiled=True)  33 us
    all_to_all x1, blocking collectives, body(): pieces = lax.all_to_all(pieces, LINE, 0, 0, tiled=True)  27.7 us
    all_to_all x1, starting transfers between devices, body(): x = lax.all_to_all(acts[:, 0], SP, 0, 0, tiled=True)  13.1 us
    all_to_all x1, waiting for transfers between devices, body(): stats = lax.all_to_all(stats, SP, 0, 0, tiled=True)  11.5 us
    all_to_all x1, waiting for transfers between devices, body(): x = lax.all_to_all(acts[:, 0], SP, 0, 0, tiled=True)  10.7 us
    ppermute x1, starting transfers between devices, body(): other = lax.ppermute(other, 'core', [(0, 1), (1, 0)])  8.71 us
    all_to_all x1, waiting for transfers between devices, body(): whole = lax.all_to_all(summed, PAIR, 0, 0, tiled=True)  8.55 us
    pallas_call x9, Pallas kernels, call(): pl.pallas_call(kernel, out_shape=outs, in_specs=[VMEM] * len(args), out_s...  7.31 us
  transfers between devices with their start and end apart: 4, of which 3 were waited for; matrix products, arithmetic and copies ran while one was open for 2% of the time, Pallas kernels for 3%

profile of v5, /device:TPU:1, one launch (start us, length us, event | category | flops | bytes accessed | tf_op | source)
XLA Modules:
  0.0 138.3 jit_solution(2819122924692933785)
XLA Ops:
  0.6 13.1 %all-to-all-start = ((bf16[16,16,728]{2,1,0:T(8,128)(2,1)}), bf16[16,16,728]{2,1,0:T(8,128)(2,1)S(1)}, u32[]{:S(2)}, u32[]{:S(2)}) async-start(bf16[16,16,728]{2,1,0:T(8,128)(2,1)} %bitcast.11), calls=%async_computation | async-start | bytes 786432 | tf_op jit(solution)/shard_map/all_to_all | solution.py:202
  13.8 0.7 broadcast_in_dim.12.refs_3_
  14.5 0.7 broadcast_in_dim.13.refs_4_
  15.2 1.2 copy-done
  16.4 1.0 copy-done.2
  17.4 0.8 copy-done.4
  18.2 0.1 stage.1
  18.3 10.7 %all-to-all-done.x_ref = bf16[16,16,728]{2,1,0:T(8,128)(2,1)S(1)} async-done(((bf16[16,16,728]{2,1,0:T(8,128)(2,1)}), bf16[16,16,728]{2,1,0:T(8,128)(2,1)S(1)}, u32[]{:S(2)}, u32[]{:S(2)}) %all-to-all-start) | async-done | bytes 372768 | tf_op jit(solution)/shard_map/all_to_all | solution.py:202
  28.9 1.8 %forward.1 = (bf16[256,728]{1,0:T(8,128)(2,1)}, f32[256,728]{1,0:T(8,128)S(1)}, f32[16,4,728]{2,1,0:T(4,128)}) custom-call(bf16[16,16,728]{2,1,0:T(8,128)(2,1)S(1)} %all-to-all-done.x_ref, bf16[16,16,728]{2,1,0:T(8,128)(2,1)S(1)} %get-tuple-element.16.g_ref, f32[3,3,728]{2,1,0:T(4,128)S(1)} %get-tuple-element.17.k_ref, ...), custom_call_target="tpu_custom_call" | custom-call | flops 271351808 | bytes 3136224 | tf_op jit(solution)/shard_map/forward/pallas_call | solution.py:25
  30.8 3.7 %all-to-all-start.1 = ((f32[16,4,728]{2,1,0:T(4,128)}), f32[16,4,728]{2,1,0:T(4,128)S(1)}, u32[]{:S(2)}, u32[]{:S(2)}) async-start(f32[16,4,728]{2,1,0:T(4,128)} %get-tuple-element.20), calls=%async_computation.1 | async-start | bytes 393216 | tf_op jit(solution)/shard_map/all_to_all | solution.py:208
  34.4 1.6 %pick.1.refs_4_.t_ref = bf16[768,256]{1,0:T(8,128)(2,1)S(1)} custom-call(bf16[256,728]{1,0:T(8,128)(2,1)} %get-tuple-element.22.refs_0_), custom_call_target="tpu_custom_call" | custom-call | flops 286261248 | bytes 765952 | tf_op jit(solution)/shard_map/pick/pallas_call | solution.py:25
  36.0 0.0 copy-start.1
  36.0 0.0 copy-start.5
  36.0 11.5 %all-to-all-done.1.refs_0_ = f32[16,4,728]{2,1,0:T(4,128)S(1)} async-done(((f32[16,4,728]{2,1,0:T(4,128)}), f32[16,4,728]{2,1,0:T(4,128)S(1)}, u32[]{:S(2)}, u32[]{:S(2)}) %all-to-all-start.1) | async-done | bytes 186400 | tf_op jit(solution)/shard_map/all_to_all | solution.py:208
  47.6 0.0 copy-done.3
  47.6 0.6 project.1
  48.2 8.7 %collective-permute-start = (bf16[16,24,728]{2,1,0:T(8,128)(2,1)S(1)}, bf16[16,24,728]{2,1,0:T(8,128)(2,1)S(1)}, u32[]{:S(2)}, u32[]{:S(2)}) collective-permute-start(bf16[16,24,728]{2,1,0:T(8,128)(2,1)S(1)} %get-tuple-element.27), channel_id=1, source_target_pairs={{0,16},{16,0},{1,17},{17,1},{2,18},{18,2},{3,19},{19,3},{4,20},{20... | collective-permute-start | bytes 1677320 | tf_op jit(solution)/shard_map/ppermute | solution.py:218
  56.9 0.0 copy-done.1
  56.9 2.1 %input.1 = (f32[384,728]{1,0:T(8,128)S(1)}, bf16[16,16,728]{2,1,0:T(8,128)(2,1)S(1)}, f32[256,728]{1,0:T(8,128)}) custom-call(bf16[256,728]{1,0:T(8,128)(2,1)S(1)} %get-tuple-element.25.dp_ref, bf16[768,256]{1,0:T(8,128)(2,1)S(1)} %pick.1.refs_4_.t_ref, bf16[728,728]{1,0:T(8,128)(2,1)S(1)} %copy-done.1, f32[3,3,728]{2,1,0:T(4,128)S(1)} %copy-done.5, ...), custom_call_target="tpu_custom_call" | custom-call | flops 542703616 | bytes 4834016 | tf_op jit(solution)/shard_map/input/pallas_call | solution.py:25
  59.0 0.0 collective-permute-done.r_ref
  59.0 0.1 pack.1
  59.1 33.0 %all_to_all.25.b_ref = bf16[16,40,728]{2,1,0:T(8,128)(2,1)S(1)} all-to-all(bf16[16,40,728]{2,1,0:T(8,128)(2,1)S(1)} %pack.1), channel_id=1, replica_groups=mesh['yl'=4,'z'=8,'core'=2,'x'=8,'yh'=2] {'x','yh'}, dimensions={0} | all-to-all | bytes 1863680 | tf_op jit(solution)/shard_map/all_to_all | solution.py:227
  92.1 0.1 slice.19
  92.2 27.7 %all_to_all.26.b_ref = bf16[32,3,728]{2,1,0:T(4,128)(2,1)S(1)} all-to-all(bf16[32,3,728]{2,1,0:T(4,128)(2,1)S(1)} %slice.19), channel_id=1, replica_groups=mesh['yl'=4,'z'=8,'core'=2,'x'=8,'yh'=2] {'yl','z'}, dimensions={0} | all-to-all | bytes 279552 | tf_op jit(solution)/shard_map/all_to_all | solution.py:235
  119.9 0.7 copies.1
  120.6 6.5 %all-to-all-start.4 = ((f32[16,3,728]{2,1,0:T(4,128)}), f32[16,3,728]{2,1,0:T(4,128)S(1)}, u32[]{:S(2)}, u32[]{:S(2)}) async-start(f32[16,3,728]{2,1,0:T(4,128)} %copies.1), calls=%async_computation.4 | async-start | bytes 393216 | tf_op jit(solution)/shard_map/all_to_all | solution.py:239
  127.1 0.2 output.1
  127.3 0.7 copy.11
  128.1 0.8 slice_bitcast_fusion
  128.9 8.5 %all-to-all-done.4 = f32[16,3,728]{2,1,0:T(4,128)S(1)} async-done(((f32[16,3,728]{2,1,0:T(4,128)}), f32[16,3,728]{2,1,0:T(4,128)S(1)}, u32[]{:S(2)}, u32[]{:S(2)}) %all-to-all-start.4) | async-done | bytes 139808 | tf_op jit(solution)/shard_map/all_to_all | solution.py:239
  137.4 0.2 reshape.9
  137.6 0.8 slice_select_fusion
  (5 shorter events, 0.0 us)
Async XLA Ops:
  0.6 28.3 %all-to-all-start = ((bf16[16,16,728]{2,1,0:T(8,128)(2,1)}), bf16[16,16,728]{2,1,0:T(8,128)(2,1)S(1)}, u32[]{:S(2)}, u32[]{:S(2)}) async-start(bf16[16,16,728]{2,1,0:T(8,128)(2,1)} %bitcast.11), calls=%async_computation | async-start | bytes 786432 | tf_op jit(solution)/shard_map/all_to_all | solution.py:202
  15.1 1.2 copy-start
  16.4 1.0 copy-start.2
  17.4 0.8 copy-start.4
  30.8 16.8 %copy-start.3 = (bf16[1,16,16,728]{3,2,1,0:T(8,128)(2,1)S(1)}, bf16[1,16,16,728]{3,2,1,0:T(8,128)(2,1)}, u32[]{:S(2)}) copy-start(bf16[1,16,16,728]{3,2,1,0:T(8,128)(2,1)} %param.7) | copy-start | bytes 1118212
  30.8 16.8 %all-to-all-start.1 = ((f32[16,4,728]{2,1,0:T(4,128)}), f32[16,4,728]{2,1,0:T(4,128)S(1)}, u32[]{:S(2)}, u32[]{:S(2)}) async-start(f32[16,4,728]{2,1,0:T(4,128)} %get-tuple-element.20), calls=%async_computation.1 | async-start | bytes 393216 | tf_op jit(solution)/shard_map/all_to_all | solution.py:208
  36.0 20.9 %copy-start.1 = (bf16[728,728]{1,0:T(8,128)(2,1)S(1)}, bf16[728,728]{1,0:T(8,128)(2,1)}, u32[]{:S(2)}) copy-start(bf16[728,728]{1,0:T(8,128)(2,1)} %w_ref.1) | copy-start | bytes 3179908
  36.0 20.9 %copy-start.5 = (f32[3,3,728]{2,1,0:T(4,128)S(1)}, f32[3,3,728]{2,1,0:T(4,128)}, u32[]{:S(2)}) copy-start(f32[3,3,728]{2,1,0:T(4,128)} %k_ref.1) | copy-start | bytes 78628
  48.2 10.8 %collective-permute-start = (bf16[16,24,728]{2,1,0:T(8,128)(2,1)S(1)}, bf16[16,24,728]{2,1,0:T(8,128)(2,1)S(1)}, u32[]{:S(2)}, u32[]{:S(2)}) collective-permute-start(bf16[16,24,728]{2,1,0:T(8,128)(2,1)S(1)} %get-tuple-element.27), channel_id=1, source_target_pairs={{0,16},{16,0},{1,17},{17,1},{2,18},{18,2},{3,19},{19,3},{4,20},{20... | collective-permute-start | bytes 1677320 | tf_op jit(solution)/shard_map/ppermute | solution.py:218
  120.6 16.8 %all-to-all-start.4 = ((f32[16,3,728]{2,1,0:T(4,128)}), f32[16,3,728]{2,1,0:T(4,128)S(1)}, u32[]{:S(2)}, u32[]{:S(2)}) async-start(f32[16,3,728]{2,1,0:T(4,128)} %copies.1), calls=%async_computation.4 | async-start | bytes 393216 | tf_op jit(solution)/shard_map/all_to_all | solution.py:239

commit v6 on v5

--- a/solution.py
+++ b/solution.py
@@ -176,8 +176,19 @@
     total = b_ref[0].astype(F32)
     for k in range(1, b_ref.shape[0]):
         total = total + b_ref[k].astype(F32)
+    total = total.astype(BF)
     for k in range(o_ref.shape[0]):
         o_ref[k] = total
+
+
+def finish_kernel(b_ref, o_ref):
+    n, _, width = b_ref.shape
+    half = width // 2
+    odd = lax.axis_index("yh") == 1
+    rows = jnp.concatenate([b_ref[k].astype(F32) for k in range(n)], axis=0)
+    after = jnp.concatenate([rows[1:], rows[:1]], axis=0)
+    late = jnp.concatenate([rows[:, half:], after[:, :half]], axis=1)
+    o_ref[...] = jnp.where(odd, late, rows)
 
 
 def out(shape, dtype):
@@ -234,17 +245,13 @@
     )
     pieces = lax.all_to_all(pieces, LINE, 0, 0, tiled=True)
     (summed,) = call(
-        copies_kernel, [out((2 * blocks, each, width), F32)], "copies", width * width, pieces
+        copies_kernel, [out((2 * blocks, each, width), BF)], "copies", width * width, pieces
     )
     whole = lax.all_to_all(summed, PAIR, 0, 0, tiled=True)
-    whole = whole.reshape(-1)
-    span = width * width // n
-    shift = (lax.axis_index(SP) * span) % width
-    if (2 * span) % width == 0:
-        odd = shift != 0
-        weight_grad = jnp.where(odd, whole[width // 2 : width // 2 + span], whole[:span])
-    else:
-        weight_grad = lax.dynamic_slice(whole, (shift,), (span,))
+    (lined,) = call(
+        finish_kernel, [out((2 * half, width), F32)], "finish", width * width, whole
+    )
+    weight_grad = lined.reshape(-1)[: width * width // n]
     input_grad = packed[:, half:, :][:, None]
     return block_out[None], input_grad, weight_grad
 

time: 139 us -> 138 us (level)
  blocking collectives: 60.7 us -> 33 us
  starting transfers between devices: 32 us -> 50.2 us
  waiting for transfers between devices: 30.7 us -> 38.7 us
    all_to_all x1 -> x0, blocking collectives: 27.7 us -> none  [body(): pieces = lax.all_to_all(pieces, LINE, 0, 0, tiled=True)]
    all_to_all x0 -> x1, starting transfers between devices: none -> 18.2 us  [body(): pieces = lax.all_to_all(pieces, LINE, 0, 0, tiled=True)]
    all_to_all x0 -> x1, waiting for transfers between devices: none -> 8.8 us  [body(): pieces = lax.all_to_all(pieces, LINE, 0, 0, tiled=True)]
    pallas_call x9 -> x10, Pallas kernels: 7.31 us -> 8.05 us  [call(): pl.pallas_call(kernel, out_shape=outs, in_specs=[VMEM] * len(args), out_s...]
  transfers between devices with their start and end apart: 4 -> 5, of which waited for: 3 -> 4; matrix products, arithmetic and copies ran while one was open for 2% -> 2% of each run, Pallas kernels for 3% -> 3%
where the time goes in v6:
time: 138 us; the launch traced here: 137 us
  starting transfers between devices  50.2 us (36%)
  waiting for transfers between devices  38.7 us (28%)
  blocking collectives  33 us (24%)
  Pallas kernels  8.05 us (6%)
  local copies, waits for them, and re-layouts  6.73 us (5%)
    all_to_all x1, blocking collectives, body(): packed = lax.all_to_all(packed, SP, 0, 0, tiled=True)  33 us
    all_to_all x1, starting transfers between devices, body(): pieces = lax.all_to_all(pieces, LINE, 0, 0, tiled=True)  18.2 us
    all_to_all x1, starting transfers between devices, body(): x = lax.all_to_all(acts[:, 0], SP, 0, 0, tiled=True)  13.1 us
    all_to_all x1, waiting for transfers between devices, body(): stats = lax.all_to_all(stats, SP, 0, 0, tiled=True)  11.5 us
    all_to_all x1, waiting for transfers between devices, body(): x = lax.all_to_all(acts[:, 0], SP, 0, 0, tiled=True)  10.7 us
    all_to_all x1, waiting for transfers between devices, body(): pieces = lax.all_to_all(pieces, LINE, 0, 0, tiled=True)  8.8 us
    ppermute x1, starting transfers between devices, body(): other = lax.ppermute(other, 'core', [(0, 1), (1, 0)])  8.71 us
    pallas_call x10, Pallas kernels, call(): pl.pallas_call(kernel, out_shape=outs, in_specs=[VMEM] * len(args), out_s...  8.05 us
  transfers between devices with their start and end apart: 5, of which 4 were waited for; matrix products, arithmetic and copies ran while one was open for 2% of the time, Pallas kernels for 3%

profile of v6, /device:TPU:1, one launch (start us, length us, event | category | flops | bytes accessed | tf_op | source)
XLA Modules:
  0.0 137.4 jit_solution(10380451240844923126)
XLA Ops:
  0.6 13.1 %all-to-all-start = ((bf16[16,16,728]{2,1,0:T(8,128)(2,1)}), bf16[16,16,728]{2,1,0:T(8,128)(2,1)S(1)}, u32[]{:S(2)}, u32[]{:S(2)}) async-start(bf16[16,16,728]{2,1,0:T(8,128)(2,1)} %bitcast.11), calls=%async_computation | async-start | bytes 786432 | tf_op jit(solution)/shard_map/all_to_all | solution.py:213
  13.8 0.7 broadcast_in_dim.12.refs_3_
  14.5 0.7 broadcast_in_dim.13.refs_4_
  15.2 1.2 copy-done
  16.4 1.0 copy-done.2
  17.4 0.8 copy-done.4
  18.2 0.1 stage.1
  18.3 10.7 %all-to-all-done.x_ref = bf16[16,16,728]{2,1,0:T(8,128)(2,1)S(1)} async-done(((bf16[16,16,728]{2,1,0:T(8,128)(2,1)}), bf16[16,16,728]{2,1,0:T(8,128)(2,1)S(1)}, u32[]{:S(2)}, u32[]{:S(2)}) %all-to-all-start) | async-done | bytes 372768 | tf_op jit(solution)/shard_map/all_to_all | solution.py:213
  28.9 1.8 %forward.1 = (bf16[256,728]{1,0:T(8,128)(2,1)}, f32[256,728]{1,0:T(8,128)S(1)}, f32[16,4,728]{2,1,0:T(4,128)}) custom-call(bf16[16,16,728]{2,1,0:T(8,128)(2,1)S(1)} %all-to-all-done.x_ref, bf16[16,16,728]{2,1,0:T(8,128)(2,1)S(1)} %get-tuple-element.16.g_ref, f32[3,3,728]{2,1,0:T(4,128)S(1)} %get-tuple-element.17.k_ref, ...), custom_call_target="tpu_custom_call" | custom-call | flops 271351808 | bytes 3136224 | tf_op jit(solution)/shard_map/forward/pallas_call | solution.py:25
  30.8 3.7 %all-to-all-start.1 = ((f32[16,4,728]{2,1,0:T(4,128)}), f32[16,4,728]{2,1,0:T(4,128)S(1)}, u32[]{:S(2)}, u32[]{:S(2)}) async-start(f32[16,4,728]{2,1,0:T(4,128)} %get-tuple-element.20), calls=%async_computation.1 | async-start | bytes 393216 | tf_op jit(solution)/shard_map/all_to_all | solution.py:219
  34.4 1.6 %pick.1.refs_4_.t_ref = bf16[768,256]{1,0:T(8,128)(2,1)S(1)} custom-call(bf16[256,728]{1,0:T(8,128)(2,1)} %get-tuple-element.22.refs_0_), custom_call_target="tpu_custom_call" | custom-call | flops 286261248 | bytes 765952 | tf_op jit(solution)/shard_map/pick/pallas_call | solution.py:25
  36.0 0.0 copy-start.1
  36.0 0.0 copy-start.5
  36.0 11.5 %all-to-all-done.1.refs_0_ = f32[16,4,728]{2,1,0:T(4,128)S(1)} async-done(((f32[16,4,728]{2,1,0:T(4,128)}), f32[16,4,728]{2,1,0:T(4,128)S(1)}, u32[]{:S(2)}, u32[]{:S(2)}) %all-to-all-start.1) | async-done | bytes 186400 | tf_op jit(solution)/shard_map/all_to_all | solution.py:219
  47.6 0.6 project.1
  48.2 8.7 %collective-permute-start = (bf16[16,24,728]{2,1,0:T(8,128)(2,1)S(1)}, bf16[16,24,728]{2,1,0:T(8,128)(2,1)S(1)}, u32[]{:S(2)}, u32[]{:S(2)}) collective-permute-start(bf16[16,24,728]{2,1,0:T(8,128)(2,1)S(1)} %get-tuple-element.27), channel_id=1, source_target_pairs={{0,16},{16,0},{1,17},{17,1},{2,18},{18,2},{3,19},{19,3},{4,20},{20... | collective-permute-start | bytes 1677320 | tf_op jit(solution)/shard_map/ppermute | solution.py:229
  56.9 2.0 %input.1 = (f32[384,728]{1,0:T(8,128)S(1)}, bf16[16,16,728]{2,1,0:T(8,128)(2,1)S(1)}, f32[256,728]{1,0:T(8,128)}) custom-call(bf16[256,728]{1,0:T(8,128)(2,1)S(1)} %get-tuple-element.25.dp_ref, bf16[768,256]{1,0:T(8,128)(2,1)S(1)} %pick.1.refs_4_.t_ref, bf16[728,728]{1,0:T(8,128)(2,1)S(1)} %copy-done.1, f32[3,3,728]{2,1,0:T(4,128)S(1)} %copy-done.5, ...), custom_call_target="tpu_custom_call" | custom-call | flops 542703616 | bytes 4834016 | tf_op jit(solution)/shard_map/input/pallas_call | solution.py:25
  58.9 0.0 collective-permute-done.r_ref
  58.9 0.1 pack.1
  59.1 33.0 %all_to_all.25.b_ref = bf16[16,40,728]{2,1,0:T(8,128)(2,1)S(1)} all-to-all(bf16[16,40,728]{2,1,0:T(8,128)(2,1)S(1)} %pack.1), channel_id=1, replica_groups=mesh['yl'=4,'z'=8,'core'=2,'x'=8,'yh'=2] {'x','yh'}, dimensions={0} | all-to-all | bytes 1863680 | tf_op jit(solution)/shard_map/all_to_all | solution.py:238
  92.0 0.8 slice.12
  92.8 18.2 %all-to-all-start.3 = ((bf16[32,3,728]{2,1,0:T(4,128)(2,1)}), bf16[32,3,728]{2,1,0:T(4,128)(2,1)S(1)}, u32[]{:S(2)}, u32[]{:S(2)}) async-start(bf16[32,3,728]{2,1,0:T(4,128)(2,1)} %slice.12), calls=%async_computation.3 | async-start | bytes 393216 | tf_op jit(solution)/shard_map/all_to_all | solution.py:246
  111.0 0.2 output.1
  111.2 0.7 copy.10
  111.9 8.8 %all-to-all-done.3.b_ref = bf16[32,3,728]{2,1,0:T(4,128)(2,1)S(1)} async-done(((bf16[32,3,728]{2,1,0:T(4,128)(2,1)}), bf16[32,3,728]{2,1,0:T(4,128)(2,1)S(1)}, u32[]{:S(2)}, u32[]{:S(2)}) %all-to-all-start.3) | async-done | bytes 139808 | tf_op jit(solution)/shard_map/all_to_all | solution.py:246
  120.7 0.7 copies.1
  121.4 6.5 %all-to-all-start.4 = ((bf16[16,3,728]{2,1,0:T(4,128)(2,1)}), bf16[16,3,728]{2,1,0:T(4,128)(2,1)S(1)}, u32[]{:S(2)}, u32[]{:S(2)}) async-start(bf16[16,3,728]{2,1,0:T(4,128)(2,1)} %copies.1), calls=%async_computation.4 | async-start | bytes 196608 | tf_op jit(solution)/shard_map/all_to_all | solution.py:250
  127.9 0.8 slice_bitcast_fusion
  128.7 7.7 %all-to-all-done.4.b_ref = bf16[16,3,728]{2,1,0:T(4,128)(2,1)S(1)} async-done(((bf16[16,3,728]{2,1,0:T(4,128)(2,1)}), bf16[16,3,728]{2,1,0:T(4,128)(2,1)S(1)}, u32[]{:S(2)}, u32[]{:S(2)}) %all-to-all-start.4) | async-done | bytes 69920 | tf_op jit(solution)/shard_map/all_to_all | solution.py:250
  136.4 0.1 finish.1
  136.6 0.1 reshape.9
  136.7 0.7 slice.10
  (7 shorter events, 0.0 us)
Async XLA Ops:
  0.6 28.3 %all-to-all-start = ((bf16[16,16,728]{2,1,0:T(8,128)(2,1)}), bf16[16,16,728]{2,1,0:T(8,128)(2,1)S(1)}, u32[]{:S(2)}, u32[]{:S(2)}) async-start(bf16[16,16,728]{2,1,0:T(8,128)(2,1)} %bitcast.11), calls=%async_computation | async-start | bytes 786432 | tf_op jit(solution)/shard_map/all_to_all | solution.py:213
  15.1 1.2 copy-start
  16.4 1.0 copy-start.2
  17.4 0.8 copy-start.4
  30.8 16.8 %copy-start.3 = (bf16[1,16,16,728]{3,2,1,0:T(8,128)(2,1)S(1)}, bf16[1,16,16,728]{3,2,1,0:T(8,128)(2,1)}, u32[]{:S(2)}) copy-start(bf16[1,16,16,728]{3,2,1,0:T(8,128)(2,1)} %param.7) | copy-start | bytes 1118212
  30.8 16.8 %all-to-all-start.1 = ((f32[16,4,728]{2,1,0:T(4,128)}), f32[16,4,728]{2,1,0:T(4,128)S(1)}, u32[]{:S(2)}, u32[]{:S(2)}) async-start(f32[16,4,728]{2,1,0:T(4,128)} %get-tuple-element.20), calls=%async_computation.1 | async-start | bytes 393216 | tf_op jit(solution)/shard_map/all_to_all | solution.py:219
  36.0 20.9 %copy-start.1 = (bf16[728,728]{1,0:T(8,128)(2,1)S(1)}, bf16[728,728]{1,0:T(8,128)(2,1)}, u32[]{:S(2)}) copy-start(bf16[728,728]{1,0:T(8,128)(2,1)} %w_ref.1) | copy-start | bytes 3179908
  36.0 20.9 %copy-start.5 = (f32[3,3,728]{2,1,0:T(4,128)S(1)}, f32[3,3,728]{2,1,0:T(4,128)}, u32[]{:S(2)}) copy-start(f32[3,3,728]{2,1,0:T(4,128)} %k_ref.1) | copy-start | bytes 78628
  48.2 10.8 %collective-permute-start = (bf16[16,24,728]{2,1,0:T(8,128)(2,1)S(1)}, bf16[16,24,728]{2,1,0:T(8,128)(2,1)S(1)}, u32[]{:S(2)}, u32[]{:S(2)}) collective-permute-start(bf16[16,24,728]{2,1,0:T(8,128)(2,1)S(1)} %get-tuple-element.27), channel_id=1, source_target_pairs={{0,16},{16,0},{1,17},{17,1},{2,18},{18,2},{3,19},{19,3},{4,20},{20... | collective-permute-start | bytes 1677320 | tf_op jit(solution)/shard_map/ppermute | solution.py:229
  92.8 27.9 %all-to-all-start.3 = ((bf16[32,3,728]{2,1,0:T(4,128)(2,1)}), bf16[32,3,728]{2,1,0:T(4,128)(2,1)S(1)}, u32[]{:S(2)}, u32[]{:S(2)}) async-start(bf16[32,3,728]{2,1,0:T(4,128)(2,1)} %slice.12), calls=%async_computation.3 | async-start | bytes 393216 | tf_op jit(solution)/shard_map/all_to_all | solution.py:246
  121.4 15.0 %all-to-all-start.4 = ((bf16[16,3,728]{2,1,0:T(4,128)(2,1)}), bf16[16,3,728]{2,1,0:T(4,128)(2,1)S(1)}, u32[]{:S(2)}, u32[]{:S(2)}) async-start(bf16[16,3,728]{2,1,0:T(4,128)(2,1)} %copies.1), calls=%async_computation.4 | async-start | bytes 196608 | tf_op jit(solution)/shard_map/all_to_all | solution.py:250
